TPU v7x, 128 devices: a whole 4x4x4 slice. The times are simulated.
128 devices in a mesh: runner: 8 (over z, core), tile: 16 (over y, x).
Axes of the slice: x: 4, y: 4, z: 4, core: 2. Of those that a mesh axis runs over, the one named last changes fastest.
Arguments:
- prior_mean_fields: float32 [3, 128, 512], P(None, 'tile'), may hold values from -0.2 to 0.2
- ensemble_deviations: float32 [256, 3, 128, 512], P('runner', None, 'tile'), may hold values from -0.75 to 0.75
- obs_cell: int32 [16, 8, 256], P('tile', 'runner'), may hold values from 0 to 1535
- obs_value: float32 [16, 8, 256], P('tile', 'runner'), may hold values from -3 to 3
- obs_var: float32 [16, 8, 256], P('tile', 'runner'), may hold values from 0.02 to 0.2
Outputs:
- advanced: float32 [256, 3, 128, 512], P('runner', None, 'tile')
Inputs may be any that keep to these rules, and one draw needn't show every extreme that they name: obs_cell[t, s, o] numbers a value of slab (t, s) as field * 512 + row within the slab * 512 + column.
All inputs are finite; a program needn't handle non-finite values.
Results may differ from a plain program's by a relative error of at most 0.0001.
Values sent between devices are 32-bit elements; how exact they have to be, the bound alone decides.
No kernel may reach another device: no remote copies, remote signals or barrier semaphores. Data moves between devices by JAX's collectives and lax.ppermute only.
A program may use at most 128 MiB of HBM per device.

v0:
```python
import jax
import jax.numpy as jnp
from jax import lax
from jax.sharding import PartitionSpec as P

DB_ITERS = 3


TIME_STEP = 0.25
CORIOLIS = 0.2


def padded_2(block, sides, width):
    for axis, dim in sides:
        count = lax.axis_size(axis)
        forward = [(i, i + 1) for i in range(count - 1)]
        forward.append((count - 1, 0))
        backward = [(target, source) for source, target in forward]
        low = lax.ppermute(
            lax.slice_in_dim(block, block.shape[dim] - width, None, axis=dim), axis, forward
        )
        high = lax.ppermute(lax.slice_in_dim(block, 0, width, axis=dim), axis, backward)
        block = jnp.concatenate([low, block, high], axis=dim)
    return block


def along_x(field):
    return (
        8.0 * (jnp.roll(field, -1, -1) - jnp.roll(field, 1, -1))
        - (jnp.roll(field, -2, -1) - jnp.roll(field, 2, -1))
    ) / 12.0


def along_y(padded):
    return (8.0 * (padded[:, 3:-1] - padded[:, 1:-3]) - (padded[:, 4:] - padded[:, :-4])) / 12.0


def tendency_padded(padded):
    height = padded[:, 0]
    east_speed = padded[:, 1]
    north_speed = padded[:, 2]
    column_depth = 1.0 + height
    flux_x = column_depth * east_speed
    flux_y = column_depth * north_speed
    east_mid = east_speed[:, 2:-2]
    north_mid = north_speed[:, 2:-2]
    height_rate = -(along_x(flux_x[:, 2:-2]) + along_y(flux_y))
    east_rate = (
        -(east_mid * along_x(east_mid) + north_mid * along_y(east_speed))
        + CORIOLIS * north_mid
        - along_x(height[:, 2:-2])
    )
    north_rate = (
        -(east_mid * along_x(north_mid) + north_mid * along_y(north_speed))
        - CORIOLIS * east_mid
        - along_y(height)
    )
    return jnp.stack([height_rate, east_rate, north_rate], axis=1)


def tendency_of(state_now):
    padded = padded_2(state_now, (("tile", 2),), 2)
    return tendency_padded(padded)


def runge_kutta_update(state_now):
    slope_one = tendency_of(state_now)
    slope_two = tendency_of(state_now + 0.5 * TIME_STEP * slope_one)
    slope_three = tendency_of(state_now + 0.5 * TIME_STEP * slope_two)
    slope_four = tendency_of(state_now + TIME_STEP * slope_three)
    return state_now + TIME_STEP / 6.0 * (
        slope_one + 2.0 * slope_two + 2.0 * slope_three + slope_four
    )


def symmetric_inverse(matrix, identity):
    sym = 0.5 * (matrix + matrix.T)
    return jax.scipy.linalg.cho_solve((jnp.linalg.cholesky(sym), True), identity)


def inverse_root(matrix, iterations):
    identity = jnp.eye(matrix.shape[0], dtype=matrix.dtype)
    square_root = matrix
    inverse_part = identity
    for _ in range(iterations):
        inv_square = symmetric_inverse(square_root, identity)
        inv_inverse = symmetric_inverse(inverse_part, identity)
        square_root, inverse_part = (
            0.5 * (square_root + inv_inverse),
            0.5 * (inverse_part + inv_square),
        )
    return inverse_part


def make_transform(gram_matrix, innovation, ensemble):
    identity = jnp.eye(ensemble, dtype=gram_matrix.dtype)
    matrix = identity + gram_matrix / (ensemble - 1.0)
    root = inverse_root(matrix, DB_ITERS)
    inner = jnp.dot(root, innovation, precision=lax.Precision.HIGHEST)
    weights = jnp.dot(root, inner, precision=lax.Precision.HIGHEST) / (ensemble - 1.0)
    return root + weights[:, None]


def correct_with_observations(flat_state, columns):
    member_mean = jnp.mean(flat_state, axis=0)
    return member_mean + jnp.einsum(
        "kc,km->mc", flat_state - member_mean, columns, precision=lax.Precision.HIGHEST
    )


def per_device(prior_mean_fields, ensemble_deviations, obs_cell, obs_value, obs_var):
    runner_count = lax.axis_size("runner")
    slab_number = lax.axis_index("runner")
    members_dev, field_count, tile_rows, columns = ensemble_deviations.shape
    ensemble = members_dev * runner_count
    slab_rows = tile_rows // runner_count
    integrate_ensemble_trajectory = runge_kutta_update(
        prior_mean_fields[None] + ensemble_deviations
    )
    cell_list = obs_cell[0, 0]
    obs_values = obs_value[0, 0]
    variance = obs_var[0, 0]
    gathered = lax.all_gather(integrate_ensemble_trajectory, "runner", axis=0, tiled=True)
    flat_state = gathered.reshape(ensemble, -1)
    slab_state = lax.dynamic_slice_in_dim(gathered, slab_number * slab_rows, slab_rows, 2).reshape(
        ensemble, -1
    )
    picked = jnp.take(slab_state, cell_list, axis=1)
    mean_obs = jnp.mean(picked, axis=0)
    anomaly = picked - mean_obs
    scaled = anomaly / variance
    gram_part = jnp.einsum("ko,lo->kl", scaled, anomaly, precision=lax.Precision.HIGHEST)
    innovation_part = jnp.einsum(
        "ko,o->k", scaled, obs_values - mean_obs, precision=lax.Precision.HIGHEST
    )
    gram_matrix, innovation = lax.psum((gram_part, innovation_part), ("runner", "tile"))
    ensemble_mixing_matrix = make_transform(gram_matrix, innovation, ensemble)
    own_columns = lax.dynamic_slice_in_dim(
        ensemble_mixing_matrix, slab_number * members_dev, members_dev, 1
    )
    returned = correct_with_observations(flat_state, own_columns).reshape(
        members_dev, field_count, tile_rows, columns
    )
    return returned + TIME_STEP * tendency_of(returned)


def solution(mesh):
    placed = (
        P(None, "tile", None),
        P("runner", None, "tile", None),
        P("tile", "runner", None),
        P("tile", "runner", None),
        P("tile", "runner", None),
    )
    return jax.shard_map(
        per_device,
        mesh=mesh,
        in_specs=placed,
        out_specs=P("runner", None, "tile", None),
        check_vma=False,
    )
```

profile of v0, /device:TPU:0, one launch (start us, length us, event | category | flops | bytes accessed | tf_op | source)
XLA Modules:
  0.0 614.2 jit_solution(7606693470243739821)
XLA Ops:
  6.5 2.3 copy_add_fusion
  8.9 1.7 collective-permute-start
  10.6 3.8 collective-permute-start.1
  14.4 9.0 %collective-permute-done = f32[32,3,2,512]{3,0,2,1:T(8,128)S(1)} collective-permute-done((f32[32,3,2,512]{3,0,2,1:T(8,128)S(1)}, f32[32,3,2,512]{3,0,2,1:T(8,128)S(1)}, u32[]{:S(2)}, u32[]{:S(2)}) %collective-permute-start) | collective-permute-done | bytes 393248 | tf_op jit(solution)/shard_map/ppermute | solution.py:19
  30.5 5.5 collective-permute-start.3
  36.0 8.0 %collective-permute-done.2 = f32[32,3,2,512]{3,0,2,1:T(8,128)S(1)} collective-permute-done((f32[32,3,2,512]{3,0,2,1:T(8,128)S(1)}, f32[32,3,2,512]{3,0,2,1:T(8,128)S(1)}, u32[]{:S(2)}, u32[]{:S(2)}) %collective-permute-start.2) | collective-permute-done | bytes 393248 | tf_op jit(solution)/shard_map/ppermute | solution.py:19
  50.8 5.6 collective-permute-start.5
  56.4 7.1 %collective-permute-done.4 = f32[32,3,2,512]{3,0,2,1:T(8,128)S(1)} collective-permute-done((f32[32,3,2,512]{3,0,2,1:T(8,128)S(1)}, f32[32,3,2,512]{3,0,2,1:T(8,128)S(1)}, u32[]{:S(2)}, u32[]{:S(2)}) %collective-permute-start.4) | collective-permute-done | bytes 393248 | tf_op jit(solution)/shard_map/ppermute | solution.py:19
  70.3 5.8 collective-permute-start.7
  76.1 6.0 collective-permute-done.6
  87.5 1.8 fusion.1
  89.4 2.1 copy.360
  91.9 11.7 %cholesky.290 = f32[128,128]{1,0:T(8,128)S(1)} custom-call(f32[128,128]{1,0:T(8,128)S(1)} %cholesky.425), custom_call_target="Cholesky" | custom-call | tf_op jit(solution)/shard_map/jit(cholesky)/cholesky | solution.py:78
  103.7 9.8 %custom-call.23 = f32[1,128,128]{1,2,0:T(8,128)S(1)} custom-call(f32[1,128,128]{2,1,0:T(8,128)S(1)} %get-tuple-element.302), custom_call_target="InvertDiagBlocksLowerTriangular" | custom-call | tf_op jit(solution)/shard_map/jit(cholesky)/cholesky | solution.py:78
  114.0 11.7 %cholesky.307 = f32[128,128]{1,0:T(8,128)S(1)} custom-call(f32[128,128]{1,0:T(8,128)S(1)} %convolution_subtract_fusion.13), custom_call_target="Cholesky" | custom-call | tf_op jit(solution)/shard_map/jit(cholesky)/cholesky | solution.py:78
  127.8 4.1 while.11
  131.9 19.7 %custom-call.24 = f32[2,128,128]{1,2,0:T(8,128)S(1)} custom-call(f32[2,128,128]{2,1,0:T(8,128)S(1)} %get-tuple-element.40), custom_call_target="InvertDiagBlocksLowerTriangular" | custom-call | tf_op jit(solution)/shard_map/jit(_cho_solve)/triangular_solve | solution.py:78
  154.4 6.8 %all-gather.2.cloned.1.call-done = f32[256,3,8,512]{3,2,1,0:T(8,128)} async-done(((f32[32,3,8,512]{3,2,1,0:T(8,128)}), f32[256,3,8,512]{3,2,1,0:T(8,128)}) %all-gather.2.cloned.1.call-update) | async-done | bytes 12582928 | tf_op jit(solution)/shard_map/all_gather | solution.py:123
  161.2 6.2 %constant_dynamic-slice_fusion.5 = f32[256,3,1,512]{3,2,1,0:T(1,128)S(1)} fusion(f32[256,3,8,512]{3,2,1,0:T(8,128)} %all-gather.2.cloned.1.call-done, s32[]{:T(128)S(6)} %select_n.30), kind=kLoop, calls=%fused_computation.513 | loop fusion | bytes 3145732 | tf_op jit(solution)/shard_map/dynamic_slice | solution.py:125
  171.5 5.3 reduce_sum.18
  176.8 12.7 %copy.387 = f32[256,3,8,512]{0,3,2,1:T(8,128)} copy(f32[256,3,8,512]{3,2,1,0:T(8,128)} %all-gather.2.cloned.1.call-done) | data formatting | bytes 25165824 | tf_op jit(solution)/shard_map/all_gather | solution.py:123
  189.5 10.7 %bitcast_subtract_fusion = f32[256,12288]{0,1:T(8,128)} fusion(f32[256,3,8,512]{0,3,2,1:T(8,128)} %copy.387, f32[12288]{0:T(1024)S(1)} %bitcast.332), kind=kLoop, calls=%fused_computation.12 | loop fusion | flops 3145728 | bytes 25214976 | tf_op jit(solution)/shard_map/sub | solution.py:107
  200.5 66.0 %psum.15 = f32[256]{0:T(256)S(1)} all-reduce(f32[256]{0:T(256)S(1)} %bitcast.338), channel_id=1, replica_groups=mesh['runner'=8,'tile'=16] {'runner','tile'}, use_global_device_ids=true, to_apply=%region_7.10 | all-reduce | flops 256 | bytes 2048 | tf_op jit(solution)/shard_map/psum | solution.py:136
  266.5 48.6 %all-reduce.3.cloned.1.call-done = f32[256,256]{0,1:T(8,128)} async-done(((f32[256,256]{0,1:T(8,128)}), f32[256,256]{0,1:T(8,128)}) %all-reduce.3.cloned.1.call-update) | async-done | bytes 262160 | tf_op jit(solution)/shard_map/psum | solution.py:136
  317.5 11.7 %cholesky.256 = f32[128,128]{1,0:T(8,128)S(1)} custom-call(f32[128,128]{1,0:T(8,128)S(1)} %cholesky.422), custom_call_target="Cholesky" | custom-call | tf_op jit(solution)/shard_map/jit(cholesky)/cholesky | solution.py:78
  329.2 9.8 %custom-call.21 = f32[1,128,128]{1,2,0:T(8,128)S(1)} custom-call(f32[1,128,128]{2,1,0:T(8,128)S(1)} %get-tuple-element.310), custom_call_target="InvertDiagBlocksLowerTriangular" | custom-call | tf_op jit(solution)/shard_map/jit(cholesky)/cholesky | solution.py:78
  339.5 11.7 %cholesky.273 = f32[128,128]{1,0:T(8,128)S(1)} custom-call(f32[128,128]{1,0:T(8,128)S(1)} %convolution_subtract_fusion.14), custom_call_target="Cholesky" | custom-call | tf_op jit(solution)/shard_map/jit(cholesky)/cholesky | solution.py:78
  353.8 3.8 while.10
  357.6 19.9 %custom-call.22 = f32[2,128,128]{1,2,0:T(8,128)S(1)} custom-call(f32[2,128,128]{2,1,0:T(8,128)S(1)} %get-tuple-element.39), custom_call_target="InvertDiagBlocksLowerTriangular" | custom-call | tf_op jit(solution)/shard_map/jit(_cho_solve)/triangular_solve | solution.py:78
  380.0 11.7 %cholesky.358 = f32[128,128]{1,0:T(8,128)S(1)} custom-call(f32[128,128]{1,0:T(8,128)S(1)} %cholesky.431), custom_call_target="Cholesky" | custom-call | tf_op jit(solution)/shard_map/jit(cholesky)/cholesky | solution.py:78
  391.8 9.8 %custom-call.27 = f32[1,128,128]{1,2,0:T(8,128)S(1)} custom-call(f32[1,128,128]{2,1,0:T(8,128)S(1)} %get-tuple-element.306), custom_call_target="InvertDiagBlocksLowerTriangular" | custom-call | tf_op jit(solution)/shard_map/jit(cholesky)/cholesky | solution.py:78
  402.1 11.7 %cholesky.375 = f32[128,128]{1,0:T(8,128)S(1)} custom-call(f32[128,128]{1,0:T(8,128)S(1)} %convolution_subtract_fusion.11), custom_call_target="Cholesky" | custom-call | tf_op jit(solution)/shard_map/jit(cholesky)/cholesky | solution.py:78
  416.3 3.8 while.13
  420.2 20.1 %custom-call.28 = f32[2,128,128]{1,2,0:T(8,128)S(1)} custom-call(f32[2,128,128]{2,1,0:T(8,128)S(1)} %get-tuple-element.42), custom_call_target="InvertDiagBlocksLowerTriangular" | custom-call | tf_op jit(solution)/shard_map/jit(_cho_solve)/triangular_solve | solution.py:78
  442.8 11.7 %cholesky.392 = f32[128,128]{1,0:T(8,128)S(1)} custom-call(f32[128,128]{1,0:T(8,128)S(1)} %cholesky.434), custom_call_target="Cholesky" | custom-call | tf_op jit(solution)/shard_map/jit(cholesky)/cholesky | solution.py:78
  454.6 9.8 %custom-call.29 = f32[1,128,128]{1,2,0:T(8,128)S(1)} custom-call(f32[1,128,128]{2,1,0:T(8,128)S(1)} %get-tuple-element.294), custom_call_target="InvertDiagBlocksLowerTriangular" | custom-call | tf_op jit(solution)/shard_map/jit(cholesky)/cholesky | solution.py:78
  464.9 11.7 %cholesky.409 = f32[128,128]{1,0:T(8,128)S(1)} custom-call(f32[128,128]{1,0:T(8,128)S(1)} %convolution_subtract_fusion.10), custom_call_target="Cholesky" | custom-call | tf_op jit(solution)/shard_map/jit(cholesky)/cholesky | solution.py:78
  479.2 4.0 while.14
  483.1 19.7 %custom-call.30 = f32[2,128,128]{1,2,0:T(8,128)S(1)} custom-call(f32[2,128,128]{2,1,0:T(8,128)S(1)} %get-tuple-element.43), custom_call_target="InvertDiagBlocksLowerTriangular" | custom-call | tf_op jit(solution)/shard_map/jit(_cho_solve)/triangular_solve | solution.py:78
  504.9 11.7 %cholesky.324 = f32[128,128]{1,0:T(8,128)S(1)} custom-call(f32[128,128]{1,0:T(8,128)S(1)} %cholesky.428), custom_call_target="Cholesky" | custom-call | tf_op jit(solution)/shard_map/jit(cholesky)/cholesky | solution.py:78
  516.7 9.8 %custom-call.25 = f32[1,128,128]{1,2,0:T(8,128)S(1)} custom-call(f32[1,128,128]{2,1,0:T(8,128)S(1)} %get-tuple-element.298), custom_call_target="InvertDiagBlocksLowerTriangular" | custom-call | tf_op jit(solution)/shard_map/jit(cholesky)/cholesky | solution.py:78
  527.0 11.7 %cholesky.341 = f32[128,128]{1,0:T(8,128)S(1)} custom-call(f32[128,128]{1,0:T(8,128)S(1)} %convolution_subtract_fusion.12), custom_call_target="Cholesky" | custom-call | tf_op jit(solution)/shard_map/jit(cholesky)/cholesky | solution.py:78
  541.2 3.8 while.12
  545.1 19.9 %custom-call.26 = f32[2,128,128]{1,2,0:T(8,128)S(1)} custom-call(f32[2,128,128]{2,1,0:T(8,128)S(1)} %get-tuple-element.41), custom_call_target="InvertDiagBlocksLowerTriangular" | custom-call | tf_op jit(solution)/shard_map/jit(_cho_solve)/triangular_solve | solution.py:78
  568.0 14.2 %convolution_add_fusion = f32[32,12288]{1,0:T(8,128)S(1)} fusion(f32[256,12288]{0,1:T(8,128)} %bitcast_subtract_fusion, f32[12288]{0:T(1024)S(1)} %bitcast.333, f32[256,256]{0,1:T(8,128)S(1)} %fusion.208, s32[]{:T(128)S(6)} %select_n.33, f32[256]{0:T(256)S(1)} %broadcast_multiply_fusion), kind=kOutput, calls=%fused_computation.11 | convolution fusion | flops 1208360960 | bytes 14238724 | tf_op jit(solution)/shard_map/kc,km->mc/dot_general | solution.py:106
  584.8 4.4 collective-permute-start.9
  589.3 8.4 %collective-permute-done.8 = f32[32,3,2,512]{3,0,2,1:T(8,128)S(1)} collective-permute-done((f32[32,3,2,512]{3,0,2,1:T(8,128)S(1)}, f32[32,3,2,512]{3,0,2,1:T(8,128)S(1)}, u32[]{:S(2)}, u32[]{:S(2)}) %collective-permute-start.8) | collective-permute-done | bytes 393248 | tf_op jit(solution)/shard_map/ppermute | solution.py:19
  604.8 2.1 copy.392
  (301 shorter events, 82.7 us)
Async XLA Ops:
  6.5 154.6 %all-gather.2.cloned.1.call-start = ((), (), s32[]{:S(2)}) async-start(), calls=%async_computation | async-start | bytes 14155776 | tf_op jit(solution)/shard_map/all_gather | solution.py:123
  8.9 14.5 %collective-permute-start = (f32[32,3,2,512]{3,0,2,1:T(8,128)S(1)}, f32[32,3,2,512]{3,0,2,1:T(8,128)S(1)}, u32[]{:S(2)}, u32[]{:S(2)}) collective-permute-start(f32[32,3,2,512]{3,0,2,1:T(8,128)S(1)} %get-tuple-element.129), channel_id=1, source_target_pairs={{0,1},{1,2},{2,3},{3,4},{4,5},{5,6},{6,7},{7,8},{8,9},{9,10},{10,1... | collective-permute-start | bytes 1179656 | tf_op jit(solution)/shard_map/ppermute | solution.py:19
  10.6 12.8 %collective-permute-start.1 = (f32[32,3,2,512]{3,0,2,1:T(8,128)S(1)}, f32[32,3,2,512]{3,0,2,1:T(8,128)S(1)}, u32[]{:S(2)}, u32[]{:S(2)}) collective-permute-start(f32[32,3,2,512]{3,0,2,1:T(8,128)S(1)} %get-tuple-element.130), channel_id=1, source_target_pairs={{1,0},{2,1},{3,2},{4,3},{5,4},{6,5},{7,6},{8,7},{9,8},{10,9},{11,1... | collective-permute-start | bytes 1179656 | tf_op jit(solution)/shard_map/ppermute | solution.py:22
  27.8 1.4 copy-start
  27.8 1.4 copy-start.2
  30.4 13.6 %collective-permute-start.2 = (f32[32,3,2,512]{3,0,2,1:T(8,128)S(1)}, f32[32,3,2,512]{3,0,2,1:T(8,128)S(1)}, u32[]{:S(2)}, u32[]{:S(2)}) collective-permute-start(f32[32,3,2,512]{3,0,2,1:T(8,128)S(1)} %get-tuple-element.127), channel_id=1, source_target_pairs={{0,1},{1,2},{2,3},{3,4},{4,5},{5,6},{6,7},{7,8},{8,9},{9,10},{10,1... | collective-permute-start | bytes 1179656 | tf_op jit(solution)/shard_map/ppermute | solution.py:19
  30.5 13.6 %collective-permute-start.3 = (f32[32,3,2,512]{3,0,2,1:T(8,128)S(1)}, f32[32,3,2,512]{3,0,2,1:T(8,128)S(1)}, u32[]{:S(2)}, u32[]{:S(2)}) collective-permute-start(f32[32,3,2,512]{3,0,2,1:T(8,128)S(1)} %get-tuple-element.128), channel_id=1, source_target_pairs={{1,0},{2,1},{3,2},{4,3},{5,4},{6,5},{7,6},{8,7},{9,8},{10,9},{11,1... | collective-permute-start | bytes 1179656 | tf_op jit(solution)/shard_map/ppermute | solution.py:22
  50.7 12.8 %collective-permute-start.4 = (f32[32,3,2,512]{3,0,2,1:T(8,128)S(1)}, f32[32,3,2,512]{3,0,2,1:T(8,128)S(1)}, u32[]{:S(2)}, u32[]{:S(2)}) collective-permute-start(f32[32,3,2,512]{3,0,2,1:T(8,128)S(1)} %get-tuple-element.125), channel_id=1, source_target_pairs={{0,1},{1,2},{2,3},{3,4},{4,5},{5,6},{6,7},{7,8},{8,9},{9,10},{10,1... | collective-permute-start | bytes 1179656 | tf_op jit(solution)/shard_map/ppermute | solution.py:19
  50.8 12.7 %collective-permute-start.5 = (f32[32,3,2,512]{3,0,2,1:T(8,128)S(1)}, f32[32,3,2,512]{3,0,2,1:T(8,128)S(1)}, u32[]{:S(2)}, u32[]{:S(2)}) collective-permute-start(f32[32,3,2,512]{3,0,2,1:T(8,128)S(1)} %get-tuple-element.126), channel_id=1, source_target_pairs={{1,0},{2,1},{3,2},{4,3},{5,4},{6,5},{7,6},{8,7},{9,8},{10,9},{11,1... | collective-permute-start | bytes 1179656 | tf_op jit(solution)/shard_map/ppermute | solution.py:22
  70.2 11.9 %collective-permute-start.6 = (f32[32,3,2,512]{3,0,2,1:T(8,128)S(1)}, f32[32,3,2,512]{3,0,2,1:T(8,128)S(1)}, u32[]{:S(2)}, u32[]{:S(2)}) collective-permute-start(f32[32,3,2,512]{3,0,2,1:T(8,128)S(1)} %get-tuple-element.123), channel_id=1, source_target_pairs={{0,1},{1,2},{2,3},{3,4},{4,5},{5,6},{6,7},{7,8},{8,9},{9,10},{10,1... | collective-permute-start | bytes 1179656 | tf_op jit(solution)/shard_map/ppermute | solution.py:19
  70.3 11.9 %collective-permute-start.7 = (f32[32,3,2,512]{3,0,2,1:T(8,128)S(1)}, f32[32,3,2,512]{3,0,2,1:T(8,128)S(1)}, u32[]{:S(2)}, u32[]{:S(2)}) collective-permute-start(f32[32,3,2,512]{3,0,2,1:T(8,128)S(1)} %get-tuple-element.124), channel_id=1, source_target_pairs={{1,0},{2,1},{3,2},{4,3},{5,4},{6,5},{7,6},{8,7},{9,8},{10,9},{11,1... | collective-permute-start | bytes 1179656 | tf_op jit(solution)/shard_map/ppermute | solution.py:22
  91.5 223.7 %all-reduce.3.cloned.1.call-start = ((), (), s32[]{:S(2)}) async-start(), calls=%async_computation.1 | async-start | bytes 524288 | tf_op jit(solution)/shard_map/psum | solution.py:136
  127.7 25.3 %copy-start.4 = (s32[1,1,256]{2,1,0:T(1,128)S(1)}, s32[1,1,256]{2,1,0:T(1,128)}, u32[]{:S(2)}) copy-start(s32[1,1,256]{2,1,0:T(1,128)} %param.10) | copy-start | bytes 3076
  168.8 1.2 copy-start.5
  168.8 1.2 copy-start.6
  416.3 26.0 %copy-start.1 = (f32[256,256]{0,1:T(8,128)S(1)}, f32[256,256]{0,1:T(8,128)}, u32[]{:S(2)}) copy-start(f32[256,256]{0,1:T(8,128)} %all-reduce.3.cloned.1.call-done) | copy-start | bytes 786436
  416.3 26.0 %copy-start.3 = (f32[128,256]{0,1:T(8,128)S(1)}, f32[128,256]{0,1:T(8,128)}, u32[]{:S(2)}) copy-start(f32[128,256]{0,1:T(8,128)} %fusion.261) | copy-start | bytes 393220
  583.4 14.2 %collective-permute-start.8 = (f32[32,3,2,512]{3,0,2,1:T(8,128)S(1)}, f32[32,3,2,512]{3,0,2,1:T(8,128)S(1)}, u32[]{:S(2)}, u32[]{:S(2)}) collective-permute-start(f32[32,3,2,512]{3,0,2,1:T(8,128)S(1)} %copy.409), channel_id=1, source_target_pairs={{0,1},{1,2},{2,3},{3,4},{4,5},{5,6},{6,7},{7,8},{8,9},{9,10},{10,1... | collective-permute-start | bytes 1179656 | tf_op jit(solution)/shard_map/ppermute | solution.py:19
  584.8 13.8 %collective-permute-start.9 = (f32[32,3,2,512]{3,0,2,1:T(8,128)S(1)}, f32[32,3,2,512]{3,0,2,1:T(8,128)S(1)}, u32[]{:S(2)}, u32[]{:S(2)}) collective-permute-start(f32[32,3,2,512]{3,0,2,1:T(8,128)S(1)} %copy.410), channel_id=1, source_target_pairs={{1,0},{2,1},{3,2},{4,3},{5,4},{6,5},{7,6},{8,7},{9,8},{10,9},{11,1... | collective-permute-start | bytes 1179656 | tf_op jit(solution)/shard_map/ppermute | solution.py:22
Sparse Core Ops, SparseCore 0:
  91.6 69.5 all-gather.1
  171.6 143.4 all-reduce.2
where the time goes:
time: 621 us; the launch traced here: 614 us
  other arithmetic  311 us (50%)
  waiting for transfers between devices  94 us (15%)
  blocking collectives  66 us (11%)
  local copies, waits for them, and re-layouts  62.7 us (10%)
  matrix products  29.3 us (5%)
  starting transfers between devices  28.6 us (5%)
  between operations  21.4 us (3%)
    another operation x34, other arithmetic, symmetric_inverse(): jnp.linalg.cholesky(sym)  172 us
    another operation x11, other arithmetic, symmetric_inverse(): jax.scipy.linalg.cho_solve((jnp.linalg.cholesky(sym), True), identity)  99.3 us
    psum x1, blocking collectives, per_device(): lax.psum((gram_part, innovation_part), ('runner', 'tile'))  66 us
    psum x1, waiting for transfers between devices, per_device(): lax.psum((gram_part, innovation_part), ('runner', 'tile'))  48.6 us
    ppermute x5, waiting for transfers between devices, padded_2(): lax.ppermute(lax.slice_in_dim(block, block.shape[dim] - width, None, axis...  38.6 us
    ppermute x5, starting transfers between devices, padded_2(): lax.ppermute(lax.slice_in_dim(block, 0, width, axis=dim), axis, backward)  25.1 us
    another operation x41, local copies, waits for them, and re-layouts, symmetric_inverse(): jax.scipy.linalg.cho_solve((jnp.linalg.cholesky(sym), True), identity)  19.4 us
    dot_general x1, matrix products, correct_with_observations(): jnp.einsum('kc,km->mc', flat_state - member_mean, columns, precision=lax....  14.2 us
  transfers between devices with their start and end apart: 12, of which 7 were waited for; matrix products, arithmetic and copies ran while one was open for 15% of the time, Pallas kernels for 0%

commit v1 on v0

v1 whole, which is shorter than its diff:
```python
import functools
import math

import jax
import jax.numpy as jnp
from jax import lax
from jax.experimental import pallas as pl
from jax.experimental.pallas import tpu as pltpu
from jax.sharding import PartitionSpec as P

TIME_STEP = 0.25
CORIOLIS = 0.2
LANES = 128
ROOT2 = math.sqrt(2.0)
POLE_LOW = 3.0 - 2.0 * ROOT2
POLE_HIGH = 3.0 + 2.0 * ROOT2
SHIFT = (0.0, 1.0, POLE_LOW, POLE_HIGH)
ROOT_CONST = 0.125
ROOT_COEF = (
    0.125,
    0.5,
    2.0 * (1.0 - POLE_LOW) / (POLE_HIGH - POLE_LOW),
    2.0 * (POLE_HIGH - 1.0) / (POLE_HIGH - POLE_LOW),
)
BLOCK = 32


def start_kernel(prior_ref, dev_ref, out_ref):
    members, fields, rows, width = dev_ref.shape
    for m in range(members):
        for f in range(fields):
            for cb in range(width // LANES):
                at = ((m * fields + f) * (width // LANES) + cb) * rows
                lanes = slice(cb * LANES, (cb + 1) * LANES)
                out_ref[at : at + rows, :] = dev_ref[m, f, :, lanes] + prior_ref[f, :, lanes]


def roll_x(field, shift):
    return pltpu.roll(field, shift % field.shape[-1], axis=field.ndim - 1)


def along_x(field):
    return (8.0 / 12.0) * (roll_x(field, -1) - roll_x(field, 1)) - (1.0 / 12.0) * (
        roll_x(field, -2) - roll_x(field, 2)
    )


def along_y(low2, low1, high1, high2):
    return (8.0 / 12.0) * (high1 - low1) - (1.0 / 12.0) * (high2 - low2)


def tendency(load):
    h, u, v = (load(f, 0) for f in range(3))
    hs, us, vs = ([load(f, s) for s in (-2, -1, 1, 2)] for f in range(3))
    flux_y = [(1.0 + a) * b for a, b in zip(hs, vs)]
    height = -(along_x((1.0 + h) * u) + along_y(*flux_y))
    east = -(u * along_x(u) + v * along_y(*us)) + CORIOLIS * v - along_x(h)
    north = -(u * along_x(v) + v * along_y(*vs)) - CORIOLIS * u - along_y(*hs)
    return height, east, north


def runge_kutta_kernel(in_ref, out_ref, cur_ref, acc_ref, *, tiles, members, blocks):
    per = 3 * blocks
    grid_rows = tiles * 8

    def join(parts):
        return jnp.concatenate(parts, axis=1)

    def member_step(m, _):
        def start_of(t, f):
            return join(
                [in_ref[pl.ds(((t * members + m) * per + f * blocks + cb) * 8, 8), :] for cb in range(blocks)]
            )

        def put(side, t, f, value):
            for cb in range(blocks):
                cur_ref[side, f * blocks + cb, pl.ds(8 + t * 8, 8), :] = value[
                    :, cb * LANES : (cb + 1) * LANES
                ]

        def wrap(side):
            for j in range(per):
                cur_ref[side, j, 0:8, :] = cur_ref[side, j, grid_rows : grid_rows + 8, :]
                cur_ref[side, j, grid_rows + 8 : grid_rows + 16, :] = cur_ref[side, j, 8:16, :]

        def fill(t, _):
            for f in range(3):
                put(0, t, f, start_of(t, f))
            return 0

        lax.fori_loop(0, tiles, fill, 0)
        wrap(0)
        for stage in range(4):
            side = stage % 2

            def block_step(t, _, stage=stage, side=side):
                def load(f, shift):
                    return join(
                        [cur_ref[side, f * blocks + cb, pl.ds(8 + t * 8 + shift, 8), :] for cb in range(blocks)]
                    )

                slopes = tendency(load)
                for f in range(3):
                    start = start_of(t, f)
                    weight = TIME_STEP / 6.0 * (1.0 if stage in (0, 3) else 2.0)
                    rows = pl.ds(t * 8, 8)
                    base = start if stage == 0 else acc_ref[f, rows, :]
                    total = base + weight * slopes[f]
                    if stage < 3:
                        acc_ref[f, rows, :] = total
                        step = TIME_STEP * (1.0 if stage == 2 else 0.5)
                        put(1 - side, t, f, start + step * slopes[f])
                    else:
                        for cb in range(blocks):
                            at = t * (members * per) + m * per + f * blocks + cb
                            out_ref[pl.ds(at, 8, stride=tiles * members * per), :] = total[
                                :, cb * LANES : (cb + 1) * LANES
                            ]
                return 0

            lax.fori_loop(0, tiles, block_step, 0)
            if stage < 3:
                wrap(1 - side)
        return 0

    lax.fori_loop(0, members, member_step, 0)


def gram_kernel(in_ref, cell_ref, value_ref, var_ref, pack_ref, dev_ref, mean_ref, *, ensemble, per):
    cells = cell_ref[...]
    inv_var = 1.0 / var_ref[...]
    val_w = value_ref[...] * inv_var
    lane = lax.broadcasted_iota(jnp.int32, (cells.shape[0], LANES), 1)
    total = jnp.zeros((ensemble + 8, ensemble), jnp.float32)
    for pair in range(per // 2):
        devs, lefts = [], []
        for j in (2 * pair, 2 * pair + 1):
            hit = cells == lane + j * LANES
            w = jnp.sum(jnp.where(hit, inv_var, 0.0), axis=0, keepdims=True)
            vw = jnp.sum(jnp.where(hit, val_w, 0.0), axis=0, keepdims=True)
            full = in_ref[pl.ds(j, ensemble, stride=per), :]
            mean = jnp.sum(full, axis=0, keepdims=True) * (1.0 / ensemble)
            dev = full - mean
            dev_ref[:, j * LANES : (j + 1) * LANES] = dev
            mean_ref[:, j * LANES : (j + 1) * LANES] = jnp.broadcast_to(mean, (8, LANES))
            devs.append(dev)
            z = jnp.broadcast_to(vw - mean * w, (8, LANES))
            lefts.append(jnp.concatenate([dev * w, z], axis=0))
        total = total + lax.dot_general(
            jnp.concatenate(lefts, axis=1),
            jnp.concatenate(devs, axis=1),
            (((1,), (1,)), ((), ())),
            precision=lax.Precision.HIGHEST,
            preferred_element_type=jnp.float32,
        )
    half = ensemble // 2
    sub = lax.broadcasted_iota(jnp.int32, (half, LANES), 0)
    for a in range(2):
        for cb in range(2):
            pack_ref[pl.ds(a * 2 + cb, half, stride=5), :] = total[
                a * half : (a + 1) * half, cb * LANES : (cb + 1) * LANES
            ]
    inn = total[ensemble : ensemble + 1, :]
    pack_ref[pl.ds(4, half, stride=5), :] = jnp.where(
        sub == 0,
        jnp.broadcast_to(inn[:, :LANES], (half, LANES)),
        jnp.where(sub == 1, jnp.broadcast_to(inn[:, LANES:], (half, LANES)), 0.0),
    )


def piece_sum_kernel(in_ref, out_ref):
    count = in_ref.shape[0] // 5
    for q in range(5):
        total = jnp.sum(in_ref[pl.ds(q, count, stride=5), :], axis=0, keepdims=True)
        out_ref[pl.ds(q, count, stride=5), :] = jnp.broadcast_to(total, (count, LANES))


def split3(x):
    hi = x.astype(jnp.bfloat16)
    rest = x - hi.astype(jnp.float32)
    mid = rest.astype(jnp.bfloat16)
    low = (rest - mid.astype(jnp.float32)).astype(jnp.bfloat16)
    return hi, mid, low


def packed_inverse(packed, group):
    lane = lax.broadcasted_iota(jnp.int32, packed.shape, 1)
    sub = lax.broadcasted_iota(jnp.int32, packed.shape, 0)
    within = lane % group
    first = lane - within
    for k in range(group):
        column = jnp.take_along_axis(packed, first + k, axis=1)
        row = jnp.broadcast_to(packed[k : k + 1, :], packed.shape)
        pivot = jnp.broadcast_to(column[k : k + 1, :], packed.shape)
        inv = 1.0 / pivot
        row = jnp.where(within == k, -1.0, row) * inv
        swept = jnp.where(within == k, 0.0, packed) - column * row
        packed = jnp.where(sub == k, row, swept)
    return -packed


def root_kernel(in_ref, dev_ref, mean_ref, out_ref, work_ref, *, ensemble, per):
    half = ensemble // 2
    n = ensemble
    row_id = lax.broadcasted_iota(jnp.int32, (n, n), 0)
    lane_id = lax.broadcasted_iota(jnp.int32, (n, n), 1)
    diag = row_id == lane_id
    gram = jnp.concatenate(
        [
            jnp.concatenate([in_ref[pl.ds(a * 2 + cb, half, stride=5), :] for cb in range(2)], axis=1)
            for a in range(2)
        ],
        axis=0,
    )
    matrix = gram * (1.0 / (ensemble - 1.0))
    for s, shift in enumerate(SHIFT):
        work_ref[s] = matrix + jnp.where(diag, 1.0 + shift, 0.0)
    shifts = len(SHIFT)
    lane_small = lax.broadcasted_iota(jnp.int32, (BLOCK, LANES), 1)
    lane_wide = lax.broadcasted_iota(jnp.int32, (BLOCK, n), 1)
    row_wide = lax.broadcasted_iota(jnp.int32, (BLOCK, n), 0)
    for k in range(n // BLOCK):
        rows = [work_ref[s, k * BLOCK : (k + 1) * BLOCK, :] for s in range(shifts)]
        near = (k * BLOCK) // LANES * LANES
        packed = jnp.zeros((BLOCK, LANES), jnp.float32)
        for s in range(shifts):
            move = (BLOCK * s - (k * BLOCK - near)) % LANES
            piece = rows[s][:, near : near + LANES]
            if move:
                piece = pltpu.roll(piece, move, axis=1)
            packed = jnp.where(lane_small // BLOCK == s, piece, packed)
        inverse = packed_inverse(packed, BLOCK)
        left = jnp.concatenate(
            [jnp.where(lane_small // BLOCK == s, inverse, 0.0) for s in range(shifts)], axis=0
        )
        own = (lane_wide >= k * BLOCK) & (lane_wide < (k + 1) * BLOCK)
        minus_eye = jnp.where(lane_wide == row_wide + k * BLOCK, -1.0, 0.0)
        bars = [jnp.where(own, minus_eye, r) for r in rows]
        swept = jnp.dot(
            left,
            jnp.concatenate(bars, axis=0),
            precision=lax.Precision.HIGHEST,
            preferred_element_type=jnp.float32,
        )
        for s in range(shifts):
            z = swept[s * BLOCK : (s + 1) * BLOCK, :]
            y1, y2, y3 = split3(jnp.where(own, 0.0, z))
            r1, r2, r3 = split3(bars[s])
            update = lax.dot_general(
                jnp.concatenate([y1, y1, y2, y2, y1, y3], axis=0),
                jnp.concatenate([r1, r2, r1, r2, r3, r1], axis=0),
                (((0,), (0,)), ((), ())),
                preferred_element_type=jnp.float32,
            )
            own_all = (lane_id >= k * BLOCK) & (lane_id < (k + 1) * BLOCK)
            work_ref[s] = jnp.where(own_all, 0.0, work_ref[s]) - update
            work_ref[s, k * BLOCK : (k + 1) * BLOCK, :] = z
    root = jnp.where(diag, ROOT_CONST, 0.0)
    for s in range(shifts):
        root = root - ROOT_COEF[s] * work_ref[s]
    innovation = jnp.concatenate([in_ref[4:5, :], in_ref[9:10, :]], axis=1)
    inner = jnp.sum(root * innovation, axis=1, keepdims=True)
    weights = jnp.sum(root * inner, axis=0, keepdims=True) * (1.0 / (ensemble - 1.0))
    mixing = root + weights
    for pair in range(per // 2):
        lanes = slice(pair * 2 * LANES, (pair + 1) * 2 * LANES)
        mixed = jnp.dot(
            mixing,
            dev_ref[:, lanes],
            precision=lax.Precision.HIGHEST,
            preferred_element_type=jnp.float32,
        ) + mean_ref[0:1, lanes]
        for i in range(2):
            out_ref[pl.ds(2 * pair + i, ensemble, stride=per), :] = mixed[:, i * LANES : (i + 1) * LANES]


def advance_kernel(main_ref, low_ref, high_ref, out_ref, buf_ref, *, members, per):
    blocks = per // 3
    stride = main_ref.shape[0] // 8
    first = pl.program_id(0) * members

    def one(i, _):
        m = first + i
        for j in range(per):
            buf_ref[j, 8:16, :] = main_ref[pl.ds(m * per + j, 8, stride=stride), :]
            for r in range(2):
                buf_ref[j, 6 + r : 7 + r, :] = low_ref[pl.ds(r * stride + m * per + j, 1), :]
                buf_ref[j, 16 + r : 17 + r, :] = high_ref[pl.ds(r * stride + m * per + j, 1), :]

        def load(f, shift):
            return jnp.concatenate(
                [buf_ref[f * blocks + cb, 8 + shift : 16 + shift, :] for cb in range(blocks)], axis=1
            )

        slopes = tendency(load)
        for f in range(3):
            out_ref[i, f] = load(f, 0) + TIME_STEP * slopes[f]
        return 0

    lax.fori_loop(0, members, one, 0)


VMEM = pl.BlockSpec(memory_space=pltpu.VMEM)


def f32(*shape):
    return jax.ShapeDtypeStruct(shape, jnp.float32)


def make_start(prior, deviations):
    members, fields, rows, width = deviations.shape
    step = 8
    return pl.pallas_call(
        start_kernel,
        grid=(members // step,),
        in_specs=[
            pl.BlockSpec((fields, rows, width), lambda i: (0, 0, 0)),
            pl.BlockSpec((step, fields, rows, width), lambda i: (i, 0, 0, 0)),
        ],
        out_specs=pl.BlockSpec((step * fields * rows * width // LANES, LANES), lambda i: (i, 0)),
        out_shape=f32(members * fields * rows * width // LANES, LANES),
        name="start",
    )(prior, deviations)


def runge_kutta(rows, tiles, members, blocks):
    per = 3 * blocks
    return pl.pallas_call(
        functools.partial(runge_kutta_kernel, tiles=tiles, members=members, blocks=blocks),
        in_specs=[VMEM],
        out_specs=VMEM,
        out_shape=f32(*rows.shape),
        scratch_shapes=[
            pltpu.VMEM((2, per, tiles * 8 + 16, LANES), jnp.float32),
            pltpu.VMEM((3, tiles * 8, blocks * LANES), jnp.float32),
        ],
        name="runge_kutta",
    )(rows)


def gram_pieces(rows, cell, value, var, ensemble, per):
    return pl.pallas_call(
        functools.partial(gram_kernel, ensemble=ensemble, per=per),
        in_specs=[VMEM] * 4,
        out_specs=[VMEM] * 3,
        out_shape=[f32(ensemble // 2 * 5, LANES), f32(ensemble, per * LANES), f32(8, per * LANES)],
        name="gram",
    )(rows, cell, value, var)


def piece_sum(pieces):
    return pl.pallas_call(
        piece_sum_kernel, in_specs=[VMEM], out_specs=VMEM, out_shape=f32(*pieces.shape), name="piece_sum"
    )(pieces)


def analyse(pieces, dev, mean, ensemble, per):
    return pl.pallas_call(
        functools.partial(root_kernel, ensemble=ensemble, per=per),
        in_specs=[VMEM] * 3,
        out_specs=VMEM,
        out_shape=f32(ensemble * per, LANES),
        scratch_shapes=[pltpu.VMEM((len(SHIFT), ensemble, ensemble), jnp.float32)],
        name="analyse",
    )(pieces, dev, mean)


def advance(main, low, high, members, per):
    step = 8
    return pl.pallas_call(
        functools.partial(advance_kernel, members=step, per=per),
        grid=(members // step,),
        in_specs=[VMEM] * 3,
        out_specs=pl.BlockSpec((step, 3, 8, per // 3 * LANES), lambda i: (i, 0, 0, 0)),
        out_shape=f32(members, 3, 8, per // 3 * LANES),
        scratch_shapes=[pltpu.VMEM((per, 24, LANES), jnp.float32)],
        name="advance",
    )(main, low, high)


def exchange(rows, axes, count):
    moved = lax.all_to_all(rows.reshape(count, -1), axes, 0, 0, tiled=True)
    return moved.reshape(rows.shape)


def per_device(prior_mean_fields, ensemble_deviations, obs_cell, obs_value, obs_var):
    runners, tiles = lax.axis_size("runner"), lax.axis_size("tile")
    members_dev, _, _, width = ensemble_deviations.shape
    blocks = width // LANES
    per = 3 * blocks
    ensemble = members_dev * runners
    whole = ("runner", "tile")
    start = make_start(prior_mean_fields, ensemble_deviations)
    grids = exchange(start, "tile", tiles)
    forecast = runge_kutta(grids, tiles, members_dev // tiles, blocks)
    slab = exchange(forecast, whole, runners * tiles)
    pieces, dev, mean = gram_pieces(
        slab, obs_cell.reshape(-1, 1), obs_value.reshape(-1, 1), obs_var.reshape(-1, 1), ensemble, per
    )
    pieces = exchange(pieces, whole, runners * tiles)
    pieces = exchange(piece_sum(pieces), whole, runners * tiles)
    analysed = exchange(analyse(pieces, dev, mean, ensemble, per), "runner", runners)
    edge = 2 * members_dev * per
    forward = [(i, (i + 1) % tiles) for i in range(tiles)]
    backward = [(target, source) for source, target in forward]
    low = lax.ppermute(analysed[-edge:], "tile", forward)
    high = lax.ppermute(analysed[:edge], "tile", backward)
    return advance(analysed, low, high, members_dev, per)


def solution(mesh):
    placed = (
        P(None, "tile", None),
        P("runner", None, "tile", None),
        P("tile", "runner", None),
        P("tile", "runner", None),
        P("tile", "runner", None),
    )
    return jax.shard_map(
        per_device,
        mesh=mesh,
        in_specs=placed,
        out_specs=P("runner", None, "tile", None),
        check_vma=False,
    )
```

time: 621 us -> 208 us (0.33)
  other arithmetic: 311 us -> 0 us
  Pallas kernels: 0 us -> 70.5 us
  waiting for transfers between devices: 94 us -> 30.5 us
  local copies, waits for them, and re-layouts: 62.7 us -> 4.48 us
  matrix products: 29.3 us -> 0 us
  blocking collectives: 66 us -> 89.1 us
  between operations: 21.4 us -> 0.04 us
  starting transfers between devices: 28.6 us -> 12.6 us
    another operation x60 -> x0, other arithmetic: 281 us -> none  [the longest x34 172 us: symmetric_inverse(): jnp.linalg.cholesky(sym)]
    all_to_all x0 -> x4, blocking collectives: none -> 89.1 us  [exchange(): moved = lax.all_to_all(rows.reshape(count, -1), axes, 0, 0, tiled=True)]
    pallas_call x0 -> x6, Pallas kernels: none -> 70.5 us  [the longest x1 31.4 us: analyse(): pl.pallas_call(functools.partial(root_kernel, ensemble=ensemble, per=per)...]
    psum x1 -> x0, blocking collectives: 66 us -> none  [per_device(): lax.psum((gram_part, innovation_part), ('runner', 'tile'))]
    psum x1 -> x0, waiting for transfers between devices: 48.6 us -> none  [per_device(): lax.psum((gram_part, innovation_part), ('runner', 'tile'))]
    ppermute x10 -> x2, waiting for transfers between devices: 38.6 us -> 8.47 us  [the longest x1 8.46 us: per_device(): low = lax.ppermute(analysed[-edge:], 'tile', forward)]
    ppermute x10 -> x2, starting transfers between devices: 28.4 us -> 5.41 us  [the longest x1 4.74 us: per_device(): high = lax.ppermute(analysed[:edge], 'tile', backward)]
    all_to_all x0 -> x1, waiting for transfers between devices: none -> 22 us  [exchange(): moved = lax.all_to_all(rows.reshape(count, -1), axes, 0, 0, tiled=True)]
  transfers between devices with their start and end apart: 12 -> 3, of which waited for: 7 -> 2; matrix products, arithmetic and copies ran while one was open for 15% -> 1% of each run, Pallas kernels for 0% -> 0%
where the time goes in v1:
time: 208 us; the launch traced here: 207 us
  blocking collectives  89.1 us (43%)
  Pallas kernels  70.5 us (34%)
  waiting for transfers between devices  30.5 us (15%)
  starting transfers between devices  12.6 us (6%)
  local copies, waits for them, and re-layouts  4.48 us (2%)
    all_to_all x4, blocking collectives, exchange(): moved = lax.all_to_all(rows.reshape(count, -1), axes, 0, 0, tiled=True)  89.1 us
    pallas_call x1, Pallas kernels, analyse(): pl.pallas_call(functools.partial(root_kernel, ensemble=ensemble, per=per)...  31.4 us
    all_to_all x1, waiting for transfers between devices, exchange(): moved = lax.all_to_all(rows.reshape(count, -1), axes, 0, 0, tiled=True)  22 us
    pallas_call x1, Pallas kernels, runge_kutta(): pl.pallas_call(functools.partial(runge_kutta_kernel, tiles=tiles, members...  21.7 us
    ppermute x1, waiting for transfers between devices, per_device(): low = lax.ppermute(analysed[-edge:], 'tile', forward)  8.46 us
    pallas_call x1, Pallas kernels, advance(): pl.pallas_call(functools.partial(advance_kernel, members=step, per=per),...  7.69 us
    all_to_all x1, starting transfers between devices, exchange(): moved = lax.all_to_all(rows.reshape(count, -1), axes, 0, 0, tiled=True)  7.17 us
    ppermute x1, starting transfers between devices, per_device(): high = lax.ppermute(analysed[:edge], 'tile', backward)  4.74 us
  transfers between devices with their start and end apart: 3, of which 2 were waited for; matrix products, arithmetic and copies ran while one was open for 1% of the time, Pallas kernels for 0%

profile of v1, /device:TPU:0, one launch (start us, length us, event | category | flops | bytes accessed | tf_op | source)
XLA Modules:
  0.0 207.3 jit_solution(157666279988532428)
XLA Ops:
  0.0 3.6 %start.1 = f32[3072,128]{1,0:T(8,128)} custom-call(f32[3,8,512]{2,1,0:T(8,128)} %prior_ref.1, f32[32,3,8,512]{3,2,1,0:T(8,128)} %dev_ref.1), custom_call_target="tpu_custom_call" | custom-call | tf_op jit(solution)/shard_map/start/pallas_call | solution.py:313
  3.6 30.0 %all_to_all.45 = f32[16,1,24576]{2,1,0:T(1,128)} all-to-all(f32[16,1,24576]{2,1,0:T(1,128)} %bitcast.19), channel_id=1, replica_groups=mesh['runner'=8,'tile'=16] {'tile'}, dimensions={0} | all-to-all | bytes 3145728 | tf_op jit(solution)/shard_map/all_to_all | solution.py:382
  33.6 21.7 %runge_kutta.1 = f32[3072,128]{1,0:T(8,128)} custom-call(f32[3072,128]{1,0:T(8,128)} %bitcast.18), custom_call_target="tpu_custom_call" | custom-call | tf_op jit(solution)/shard_map/runge_kutta/pallas_call | solution.py:328
  55.3 0.0 copy-start.4
  55.3 0.0 copy-start.5
  55.3 0.0 copy-start.6
  55.3 7.2 %all-to-all-start.1 = ((f32[128,1,3072]{2,1,0:T(1,128)}), f32[128,1,3072]{2,1,0:T(1,128)S(1)}, u32[]{:S(2)}, u32[]{:S(2)}) async-start(f32[128,1,3072]{2,1,0:T(1,128)} %bitcast.16), calls=%async_computation.1 | async-start | bytes 3145728 | tf_op jit(solution)/shard_map/all_to_all | solution.py:382
  62.5 0.0 copy-done.4
  62.5 0.8 copy.11.cell_ref
  63.3 0.0 copy-done.5
  63.3 0.8 copy.12.value_ref
  64.1 0.0 copy-done.6
  64.1 0.8 copy.13.var_ref
  64.9 22.0 %all-to-all-done.1 = f32[128,1,3072]{2,1,0:T(1,128)S(1)} async-done(((f32[128,1,3072]{2,1,0:T(1,128)}), f32[128,1,3072]{2,1,0:T(1,128)S(1)}, u32[]{:S(2)}, u32[]{:S(2)}) %all-to-all-start.1) | async-done | bytes 1572896 | tf_op jit(solution)/shard_map/all_to_all | solution.py:382
  86.9 0.0 copy-start.1
  86.9 1.1 copy-done.1
  88.1 4.5 %gram.1 = (f32[640,128]{1,0:T(8,128)}, f32[256,1536]{1,0:T(8,128)}, f32[8,1536]{1,0:T(8,128)}) custom-call(f32[3072,128]{1,0:T(8,128)} %bitcast.20, s32[256,1]{1,0:T(8,128)} %copy.11.cell_ref, f32[256,1]{1,0:T(8,128)} %copy.12.value_ref, f32[256,1]{1,0:T(8,128)} %copy.13.var_ref), custom_call_target="tpu_custom_call" | custom-call | tf_op jit(solution)/shard_map/gram/pallas_call | solution.py:342
  92.5 17.0 %all_to_all.46 = f32[128,1,640]{2,1,0:T(1,128)} all-to-all(f32[128,1,640]{2,1,0:T(1,128)} %bitcast.26), channel_id=1, replica_groups=mesh['runner'=8,'tile'=16] {'runner','tile'}, dimensions={0} | all-to-all | bytes 655360 | tf_op jit(solution)/shard_map/all_to_all | solution.py:382
  109.5 1.7 piece_sum.1
  111.3 17.0 %all_to_all.47 = f32[128,1,640]{2,1,0:T(1,128)} all-to-all(f32[128,1,640]{2,1,0:T(1,128)} %bitcast.23), channel_id=1, replica_groups=mesh['runner'=8,'tile'=16] {'runner','tile'}, dimensions={0} | all-to-all | bytes 655360 | tf_op jit(solution)/shard_map/all_to_all | solution.py:382
  128.3 31.4 %analyse.1 = f32[3072,128]{1,0:T(8,128)} custom-call(f32[640,128]{1,0:T(8,128)} %bitcast.21, f32[256,1536]{1,0:T(8,128)} %get-tuple-element.9.dev_ref, f32[8,1536]{1,0:T(8,128)} %get-tuple-element.10.mean_ref), custom_call_target="tpu_custom_call" | custom-call | tf_op jit(solution)/shard_map/analyse/pallas_call | solution.py:358
  159.7 25.1 %all_to_all.48 = f32[8,1,49152]{2,1,0:T(1,128)S(1)} all-to-all(f32[8,1,49152]{2,1,0:T(1,128)} %bitcast.17), channel_id=1, replica_groups=mesh['runner'=8,'tile'=16] {'runner'}, dimensions={0} | all-to-all | bytes 3145728 | tf_op jit(solution)/shard_map/all_to_all | solution.py:382
  184.8 0.0 copy-start
  184.8 0.1 fusion
  184.9 0.7 collective-permute-start
  185.5 4.7 %collective-permute-start.1 = (f32[768,128]{1,0:T(8,128)S(1)}, f32[768,128]{1,0:T(8,128)S(1)}, u32[]{:S(2)}, u32[]{:S(2)}) collective-permute-start(f32[768,128]{1,0:T(8,128)S(1)} %bitcast.24), channel_id=1, source_target_pairs={{1,0},{2,1},{3,2},{4,3},{5,4},{6,5},{7,6},{8,7},{9,8},{10,9},{11,1... | collective-permute-start | bytes 1179656 | tf_op jit(solution)/shard_map/ppermute | solution.py:407
  190.3 8.5 %collective-permute-done.low_ref = f32[768,128]{1,0:T(8,128)S(1)} collective-permute-done((f32[768,128]{1,0:T(8,128)S(1)}, f32[768,128]{1,0:T(8,128)S(1)}, u32[]{:S(2)}, u32[]{:S(2)}) %collective-permute-start) | collective-permute-done | bytes 393248 | tf_op jit(solution)/shard_map/ppermute | solution.py:406
  198.7 0.0 copy-start.2
  198.7 0.0 collective-permute-done.1.high_ref
  198.8 0.0 copy-start.3
  198.8 0.0 copy-done
  198.8 0.7 copy-done.2
  199.5 0.1 copy-done.3
  199.6 7.7 %advance.1 = f32[32,3,8,512]{3,2,1,0:T(8,128)} custom-call(f32[3072,128]{1,0:T(8,128)} %bitcast.15, f32[768,128]{1,0:T(8,128)} %copy-done.2, f32[768,128]{1,0:T(8,128)} %copy-done.3), custom_call_target="tpu_custom_call" | custom-call | tf_op jit(solution)/shard_map/advance/pallas_call | solution.py:370
Async XLA Ops:
  55.3 7.2 %copy-start.4 = (s32[1,1,256]{2,1,0:T(1,128)S(1)}, s32[1,1,256]{2,1,0:T(1,128)}, u32[]{:S(2)}) copy-start(s32[1,1,256]{2,1,0:T(1,128)} %param.7) | copy-start | bytes 3076
  55.3 8.0 %copy-start.5 = (f32[1,1,256]{2,1,0:T(1,128)S(1)}, f32[1,1,256]{2,1,0:T(1,128)}, u32[]{:S(2)}) copy-start(f32[1,1,256]{2,1,0:T(1,128)} %param.8) | copy-start | bytes 3076
  55.3 8.8 %copy-start.6 = (f32[1,1,256]{2,1,0:T(1,128)S(1)}, f32[1,1,256]{2,1,0:T(1,128)}, u32[]{:S(2)}) copy-start(f32[1,1,256]{2,1,0:T(1,128)} %param.9) | copy-start | bytes 3076
  55.3 31.6 %all-to-all-start.1 = ((f32[128,1,3072]{2,1,0:T(1,128)}), f32[128,1,3072]{2,1,0:T(1,128)S(1)}, u32[]{:S(2)}, u32[]{:S(2)}) async-start(f32[128,1,3072]{2,1,0:T(1,128)} %bitcast.16), calls=%async_computation.1 | async-start | bytes 3145728 | tf_op jit(solution)/shard_map/all_to_all | solution.py:382
  86.9 1.1 copy-start.1
  184.8 13.9 %copy-start = (f32[8,1,49152]{2,1,0:T(1,128)}, f32[8,1,49152]{2,1,0:T(1,128)S(1)}, u32[]{:S(2)}) copy-start(f32[8,1,49152]{2,1,0:T(1,128)S(1)} %all_to_all.48) | copy-start | bytes 4718596
  184.9 13.9 %collective-permute-start = (f32[768,128]{1,0:T(8,128)S(1)}, f32[768,128]{1,0:T(8,128)S(1)}, u32[]{:S(2)}, u32[]{:S(2)}) collective-permute-start(f32[768,128]{1,0:T(8,128)S(1)} %bitcast.25), channel_id=1, source_target_pairs={{0,1},{1,2},{2,3},{3,4},{4,5},{5,6},{6,7},{7,8},{8,9},{9,10},{10,1... | collective-permute-start | bytes 1179656 | tf_op jit(solution)/shard_map/ppermute | solution.py:406
  185.5 13.2 %collective-permute-start.1 = (f32[768,128]{1,0:T(8,128)S(1)}, f32[768,128]{1,0:T(8,128)S(1)}, u32[]{:S(2)}, u32[]{:S(2)}) collective-permute-start(f32[768,128]{1,0:T(8,128)S(1)} %bitcast.24), channel_id=1, source_target_pairs={{1,0},{2,1},{3,2},{4,3},{5,4},{6,5},{7,6},{8,7},{9,8},{10,9},{11,1... | collective-permute-start | bytes 1179656 | tf_op jit(solution)/shard_map/ppermute | solution.py:407
  198.7 0.7 copy-start.2
  198.8 0.9 copy-start.3

commit v2 on v1

--- a/solution.py
+++ b/solution.py
@@ -23,6 +23,7 @@
     2.0 * (POLE_HIGH - 1.0) / (POLE_HIGH - POLE_LOW),
 )
 BLOCK = 32
+PANEL = 16
 
 
 def start_kernel(prior_ref, dev_ref, out_ref):
@@ -40,87 +41,93 @@
 
 
 def along_x(field):
-    return (8.0 / 12.0) * (roll_x(field, -1) - roll_x(field, 1)) - (1.0 / 12.0) * (
-        roll_x(field, -2) - roll_x(field, 2)
-    )
-
-
-def along_y(low2, low1, high1, high2):
-    return (8.0 / 12.0) * (high1 - low1) - (1.0 / 12.0) * (high2 - low2)
+    return (roll_x(field, -1) - roll_x(field, 1)) - 0.125 * (roll_x(field, -2) - roll_x(field, 2))
+
+
+def along_y(load, f):
+    return (load(f, 1) - load(f, -1)) - 0.125 * (load(f, 2) - load(f, -2))
+
+
+SLOPE = 8.0 / 12.0
 
 
 def tendency(load):
     h, u, v = (load(f, 0) for f in range(3))
-    hs, us, vs = ([load(f, s) for s in (-2, -1, 1, 2)] for f in range(3))
-    flux_y = [(1.0 + a) * b for a, b in zip(hs, vs)]
-    height = -(along_x((1.0 + h) * u) + along_y(*flux_y))
-    east = -(u * along_x(u) + v * along_y(*us)) + CORIOLIS * v - along_x(h)
-    north = -(u * along_x(v) + v * along_y(*vs)) - CORIOLIS * u - along_y(*hs)
+    height = -SLOPE * (along_x((1.0 + h) * u) + along_y(load, 3))
+    east = CORIOLIS * v - SLOPE * (u * along_x(u) + v * along_y(load, 1) + along_x(h))
+    north = -CORIOLIS * u - SLOPE * (u * along_x(v) + v * along_y(load, 2) + along_y(load, 0))
     return height, east, north
 
 
-def runge_kutta_kernel(in_ref, out_ref, cur_ref, acc_ref, *, tiles, members, blocks):
+UNROLL = 4
+
+
+def runge_kutta_kernel(in_ref, out_ref, even_ref, odd_ref, acc_ref, *, tiles, members, blocks):
     per = 3 * blocks
     grid_rows = tiles * 8
-
-    def join(parts):
-        return jnp.concatenate(parts, axis=1)
+    sides = (even_ref, odd_ref)
+
+    def split(value):
+        return [value[:, cb * LANES : (cb + 1) * LANES] for cb in range(blocks)]
+
+    def every_tile(step):
+        def some(i, _):
+            for r in range(UNROLL):
+                step(i * UNROLL + r)
+            return 0
+
+        lax.fori_loop(0, tiles // UNROLL, some, 0)
 
     def member_step(m, _):
         def start_of(t, f):
-            return join(
-                [in_ref[pl.ds(((t * members + m) * per + f * blocks + cb) * 8, 8), :] for cb in range(blocks)]
+            return jnp.concatenate(
+                [in_ref[pl.ds(((t * members + m) * per + f * blocks + cb) * 8, 8), :] for cb in range(blocks)],
+                axis=1,
             )
 
-        def put(side, t, f, value):
-            for cb in range(blocks):
-                cur_ref[side, f * blocks + cb, pl.ds(8 + t * 8, 8), :] = value[
-                    :, cb * LANES : (cb + 1) * LANES
-                ]
-
-        def wrap(side):
-            for j in range(per):
-                cur_ref[side, j, 0:8, :] = cur_ref[side, j, grid_rows : grid_rows + 8, :]
-                cur_ref[side, j, grid_rows + 8 : grid_rows + 16, :] = cur_ref[side, j, 8:16, :]
-
-        def fill(t, _):
-            for f in range(3):
-                put(0, t, f, start_of(t, f))
-            return 0
-
-        lax.fori_loop(0, tiles, fill, 0)
-        wrap(0)
+        def put(ref, t, values):
+            flux = (1.0 + values[0]) * values[2]
+            for f, value in enumerate((*values, flux)):
+                for cb, part in enumerate(split(value)):
+                    ref[f * blocks + cb, pl.ds(8 + t * 8, 8), :] = part
+
+        def wrap(ref):
+            for j in range(4 * blocks):
+                ref[j, 0:8, :] = ref[j, grid_rows : grid_rows + 8, :]
+                ref[j, grid_rows + 8 : grid_rows + 16, :] = ref[j, 8:16, :]
+
+        every_tile(lambda t: put(even_ref, t, [start_of(t, f) for f in range(3)]))
+        wrap(even_ref)
         for stage in range(4):
-            side = stage % 2
-
-            def block_step(t, _, stage=stage, side=side):
+            here, there = sides[stage % 2], sides[1 - stage % 2]
+
+            def step(t, stage=stage, here=here, there=there):
                 def load(f, shift):
-                    return join(
-                        [cur_ref[side, f * blocks + cb, pl.ds(8 + t * 8 + shift, 8), :] for cb in range(blocks)]
+                    return jnp.concatenate(
+                        [here[f * blocks + cb, pl.ds(8 + t * 8 + shift, 8), :] for cb in range(blocks)],
+                        axis=1,
                     )
 
                 slopes = tendency(load)
+                rows = pl.ds(t * 8, 8)
+                nexts = []
                 for f in range(3):
                     start = start_of(t, f)
                     weight = TIME_STEP / 6.0 * (1.0 if stage in (0, 3) else 2.0)
-                    rows = pl.ds(t * 8, 8)
-                    base = start if stage == 0 else acc_ref[f, rows, :]
-                    total = base + weight * slopes[f]
+                    total = (start if stage == 0 else acc_ref[f, rows, :]) + weight * slopes[f]
                     if stage < 3:
                         acc_ref[f, rows, :] = total
-                        step = TIME_STEP * (1.0 if stage == 2 else 0.5)
-                        put(1 - side, t, f, start + step * slopes[f])
+                        nexts.append(start + TIME_STEP * (1.0 if stage == 2 else 0.5) * slopes[f])
                     else:
-                        for cb in range(blocks):
+                        for cb, part in enumerate(split(total)):
                             at = t * (members * per) + m * per + f * blocks + cb
-                            out_ref[pl.ds(at, 8, stride=tiles * members * per), :] = total[
-                                :, cb * LANES : (cb + 1) * LANES
-                            ]
-                return 0
-
-            lax.fori_loop(0, tiles, block_step, 0)
+                            out_ref[pl.ds(at, 8, stride=tiles * members * per), :] = part
+                if stage < 3:
+                    put(there, t, nexts)
+
+            every_tile(step)
             if stage < 3:
-                wrap(1 - side)
+                wrap(there)
         return 0
 
     lax.fori_loop(0, members, member_step, 0)
@@ -184,19 +191,33 @@
 
 
 def packed_inverse(packed, group):
-    lane = lax.broadcasted_iota(jnp.int32, packed.shape, 1)
-    sub = lax.broadcasted_iota(jnp.int32, packed.shape, 0)
+    shape = (8, LANES)
+    lane = lax.broadcasted_iota(jnp.int32, shape, 1)
+    sub = lax.broadcasted_iota(jnp.int32, shape, 0)
     within = lane % group
     first = lane - within
-    for k in range(group):
-        column = jnp.take_along_axis(packed, first + k, axis=1)
-        row = jnp.broadcast_to(packed[k : k + 1, :], packed.shape)
-        pivot = jnp.broadcast_to(column[k : k + 1, :], packed.shape)
-        inv = 1.0 / pivot
-        row = jnp.where(within == k, -1.0, row) * inv
-        swept = jnp.where(within == k, 0.0, packed) - column * row
-        packed = jnp.where(sub == k, row, swept)
-    return -packed
+    count = group // 8
+    rows = [packed[8 * i : 8 * i + 8, :] for i in range(count)]
+
+    def spread(parts, k):
+        return jnp.broadcast_to(parts[k // 8][k % 8 : k % 8 + 1, :], shape)
+
+    def sweep(parts, column, k, row):
+        out = [part - c * row for part, c in zip(parts, column)]
+        out[k // 8] = jnp.where(sub == k % 8, row, out[k // 8])
+        return out
+
+    for k0 in range(0, group, PANEL):
+        panel = range(k0, k0 + PANEL)
+        columns = {k: [jnp.take_along_axis(part, first + k, axis=1) for part in rows] for k in panel}
+        for k in panel:
+            column = columns.pop(k)
+            inv = 1.0 / spread(column, k)
+            for j in columns:
+                columns[j] = sweep(columns[j], column, k, spread(columns[j], k) * inv)
+            row = jnp.where(within == k, -1.0, spread(rows, k)) * inv
+            rows = sweep([jnp.where(within == k, 0.0, part) for part in rows], column, k, row)
+    return jnp.concatenate(rows, axis=0)
 
 
 def root_kernel(in_ref, dev_ref, mean_ref, out_ref, work_ref, *, ensemble, per):
@@ -231,7 +252,7 @@
             packed = jnp.where(lane_small // BLOCK == s, piece, packed)
         inverse = packed_inverse(packed, BLOCK)
         left = jnp.concatenate(
-            [jnp.where(lane_small // BLOCK == s, inverse, 0.0) for s in range(shifts)], axis=0
+            [jnp.where(lane_small // BLOCK == s, -inverse, 0.0) for s in range(shifts)], axis=0
         )
         own = (lane_wide >= k * BLOCK) & (lane_wide < (k + 1) * BLOCK)
         minus_eye = jnp.where(lane_wide == row_wide + k * BLOCK, -1.0, 0.0)
@@ -279,25 +300,29 @@
     stride = main_ref.shape[0] // 8
     first = pl.program_id(0) * members
 
-    def one(i, _):
+    def one(i, slot):
         m = first + i
-        for j in range(per):
-            buf_ref[j, 8:16, :] = main_ref[pl.ds(m * per + j, 8, stride=stride), :]
-            for r in range(2):
-                buf_ref[j, 6 + r : 7 + r, :] = low_ref[pl.ds(r * stride + m * per + j, 1), :]
-                buf_ref[j, 16 + r : 17 + r, :] = high_ref[pl.ds(r * stride + m * per + j, 1), :]
+        for at, ref, count in ((6, low_ref, 2), (8, main_ref, 8), (16, high_ref, 2)):
+            parts = [ref[pl.ds(m * per + j, count, stride=stride), :] for j in range(per)]
+            parts += [(1.0 + parts[cb]) * parts[2 * blocks + cb] for cb in range(blocks)]
+            for j, part in enumerate(parts):
+                buf_ref[slot, j, at : at + count, :] = part
 
         def load(f, shift):
             return jnp.concatenate(
-                [buf_ref[f * blocks + cb, 8 + shift : 16 + shift, :] for cb in range(blocks)], axis=1
+                [buf_ref[slot, f * blocks + cb, 8 + shift : 16 + shift, :] for cb in range(blocks)], axis=1
             )
 
         slopes = tendency(load)
         for f in range(3):
             out_ref[i, f] = load(f, 0) + TIME_STEP * slopes[f]
+
+    def some(i, _):
+        for r in range(UNROLL):
+            one(i * UNROLL + r, r)
         return 0
 
-    lax.fori_loop(0, members, one, 0)
+    lax.fori_loop(0, members // UNROLL, some, 0)
 
 
 VMEM = pl.BlockSpec(memory_space=pltpu.VMEM)
@@ -309,7 +334,7 @@
 
 def make_start(prior, deviations):
     members, fields, rows, width = deviations.shape
-    step = 8
+    step = 16
     return pl.pallas_call(
         start_kernel,
         grid=(members // step,),
@@ -331,7 +356,8 @@
         out_specs=VMEM,
         out_shape=f32(*rows.shape),
         scratch_shapes=[
-            pltpu.VMEM((2, per, tiles * 8 + 16, LANES), jnp.float32),
+            pltpu.VMEM((4 * blocks, tiles * 8 + 16, LANES), jnp.float32),
+            pltpu.VMEM((4 * blocks, tiles * 8 + 16, LANES), jnp.float32),
             pltpu.VMEM((3, tiles * 8, blocks * LANES), jnp.float32),
         ],
         name="runge_kutta",
@@ -373,7 +399,7 @@
         in_specs=[VMEM] * 3,
         out_specs=pl.BlockSpec((step, 3, 8, per // 3 * LANES), lambda i: (i, 0, 0, 0)),
         out_shape=f32(members, 3, 8, per // 3 * LANES),
-        scratch_shapes=[pltpu.VMEM((per, 24, LANES), jnp.float32)],
+        scratch_shapes=[pltpu.VMEM((UNROLL, per // 3 * 4, 24, LANES), jnp.float32)],
         name="advance",
     )(main, low, high)
 

time: 208 us -> 181 us (0.87)
  Pallas kernels: 70.5 us -> 43.5 us
    pallas_call x1, Pallas kernels: 31.4 us -> 15.5 us  [analyse(): pl.pallas_call(functools.partial(root_kernel, ensemble=ensemble, per=per)...]
    pallas_call x1, Pallas kernels: 21.7 us -> 14.1 us  [runge_kutta(): pl.pallas_call(functools.partial(runge_kutta_kernel, tiles=tiles, members...]
    pallas_call x1, Pallas kernels: 7.69 us -> 5.38 us  [advance(): pl.pallas_call(functools.partial(advance_kernel, members=step, per=per),...]
where the time goes in v2:
time: 181 us; the launch traced here: 180 us
  blocking collectives  89.1 us (49%)
  Pallas kernels  43.5 us (24%)
  waiting for transfers between devices  30.5 us (17%)
  starting transfers between devices  12.6 us (7%)
  local copies, waits for them, and re-layouts  4.48 us (2%)
    all_to_all x4, blocking collectives, exchange(): moved = lax.all_to_all(rows.reshape(count, -1), axes, 0, 0, tiled=True)  89.1 us
    all_to_all x1, waiting for transfers between devices, exchange(): moved = lax.all_to_all(rows.reshape(count, -1), axes, 0, 0, tiled=True)  22 us
    pallas_call x1, Pallas kernels, analyse(): pl.pallas_call(functools.partial(root_kernel, ensemble=ensemble, per=per)...  15.5 us
    pallas_call x1, Pallas kernels, runge_kutta(): pl.pallas_call(functools.partial(runge_kutta_kernel, tiles=tiles, members...  14.1 us
    ppermute x1, waiting for transfers between devices, per_device(): low = lax.ppermute(analysed[-edge:], 'tile', forward)  8.46 us
    all_to_all x1, starting transfers between devices, exchange(): moved = lax.all_to_all(rows.reshape(count, -1), axes, 0, 0, tiled=True)  7.17 us
    pallas_call x1, Pallas kernels, advance(): pl.pallas_call(functools.partial(advance_kernel, members=step, per=per),...  5.38 us
    ppermute x1, starting transfers between devices, per_device(): high = lax.ppermute(analysed[:edge], 'tile', backward)  4.73 us
  transfers between devices with their start and end apart: 3, of which 2 were waited for; matrix products, arithmetic and copies ran while one was open for 1% of the time, Pallas kernels for 0%

profile of v2, /device:TPU:0, one launch (start us, length us, event | category | flops | bytes accessed | tf_op | source)
XLA Modules:
  0.0 180.3 jit_solution(6903823655981879726)
XLA Ops:
  0.0 2.3 %start.1 = f32[3072,128]{1,0:T(8,128)} custom-call(f32[3,8,512]{2,1,0:T(8,128)} %prior_ref.1, f32[32,3,8,512]{3,2,1,0:T(8,128)} %dev_ref.1), custom_call_target="tpu_custom_call" | custom-call | tf_op jit(solution)/shard_map/start/pallas_call | solution.py:338
  2.3 30.0 %all_to_all.45 = f32[16,1,24576]{2,1,0:T(1,128)} all-to-all(f32[16,1,24576]{2,1,0:T(1,128)} %bitcast.19), channel_id=1, replica_groups=mesh['runner'=8,'tile'=16] {'tile'}, dimensions={0} | all-to-all | bytes 3145728 | tf_op jit(solution)/shard_map/all_to_all | solution.py:408
  32.3 14.1 %runge_kutta.1 = f32[3072,128]{1,0:T(8,128)} custom-call(f32[3072,128]{1,0:T(8,128)} %bitcast.18), custom_call_target="tpu_custom_call" | custom-call | tf_op jit(solution)/shard_map/runge_kutta/pallas_call | solution.py:353
  46.4 0.0 copy-start.4
  46.4 0.0 copy-start.5
  46.4 0.0 copy-start.6
  46.4 7.2 %all-to-all-start.1 = ((f32[128,1,3072]{2,1,0:T(1,128)}), f32[128,1,3072]{2,1,0:T(1,128)S(1)}, u32[]{:S(2)}, u32[]{:S(2)}) async-start(f32[128,1,3072]{2,1,0:T(1,128)} %bitcast.16), calls=%async_computation.1 | async-start | bytes 3145728 | tf_op jit(solution)/shard_map/all_to_all | solution.py:408
  53.6 0.0 copy-done.4
  53.6 0.8 copy.11.cell_ref
  54.4 0.0 copy-done.5
  54.4 0.8 copy.12.value_ref
  55.2 0.0 copy-done.6
  55.2 0.8 copy.13.var_ref
  56.0 22.0 %all-to-all-done.1 = f32[128,1,3072]{2,1,0:T(1,128)S(1)} async-done(((f32[128,1,3072]{2,1,0:T(1,128)}), f32[128,1,3072]{2,1,0:T(1,128)S(1)}, u32[]{:S(2)}, u32[]{:S(2)}) %all-to-all-start.1) | async-done | bytes 1572896 | tf_op jit(solution)/shard_map/all_to_all | solution.py:408
  78.1 0.0 copy-start.1
  78.1 1.1 copy-done.1
  79.2 4.5 %gram.1 = (f32[640,128]{1,0:T(8,128)}, f32[256,1536]{1,0:T(8,128)}, f32[8,1536]{1,0:T(8,128)}) custom-call(f32[3072,128]{1,0:T(8,128)} %bitcast.20, s32[256,1]{1,0:T(8,128)} %copy.11.cell_ref, f32[256,1]{1,0:T(8,128)} %copy.12.value_ref, f32[256,1]{1,0:T(8,128)} %copy.13.var_ref), custom_call_target="tpu_custom_call" | custom-call | tf_op jit(solution)/shard_map/gram/pallas_call | solution.py:368
  83.7 17.0 %all_to_all.46 = f32[128,1,640]{2,1,0:T(1,128)} all-to-all(f32[128,1,640]{2,1,0:T(1,128)} %bitcast.26), channel_id=1, replica_groups=mesh['runner'=8,'tile'=16] {'runner','tile'}, dimensions={0} | all-to-all | bytes 655360 | tf_op jit(solution)/shard_map/all_to_all | solution.py:408
  100.7 1.7 piece_sum.1
  102.4 17.0 %all_to_all.47 = f32[128,1,640]{2,1,0:T(1,128)} all-to-all(f32[128,1,640]{2,1,0:T(1,128)} %bitcast.23), channel_id=1, replica_groups=mesh['runner'=8,'tile'=16] {'runner','tile'}, dimensions={0} | all-to-all | bytes 655360 | tf_op jit(solution)/shard_map/all_to_all | solution.py:408
  119.5 15.5 %analyse.1 = f32[3072,128]{1,0:T(8,128)} custom-call(f32[640,128]{1,0:T(8,128)} %bitcast.21, f32[256,1536]{1,0:T(8,128)} %get-tuple-element.9.dev_ref, f32[8,1536]{1,0:T(8,128)} %get-tuple-element.10.mean_ref), custom_call_target="tpu_custom_call" | custom-call | tf_op jit(solution)/shard_map/analyse/pallas_call | solution.py:384
  135.0 25.1 %all_to_all.48 = f32[8,1,49152]{2,1,0:T(1,128)S(1)} all-to-all(f32[8,1,49152]{2,1,0:T(1,128)} %bitcast.17), channel_id=1, replica_groups=mesh['runner'=8,'tile'=16] {'runner'}, dimensions={0} | all-to-all | bytes 3145728 | tf_op jit(solution)/shard_map/all_to_all | solution.py:408
  160.1 0.0 copy-start
  160.1 0.1 fusion
  160.1 0.7 collective-permute-start
  160.8 4.7 %collective-permute-start.1 = (f32[768,128]{1,0:T(8,128)S(1)}, f32[768,128]{1,0:T(8,128)S(1)}, u32[]{:S(2)}, u32[]{:S(2)}) collective-permute-start(f32[768,128]{1,0:T(8,128)S(1)} %bitcast.24), channel_id=1, source_target_pairs={{1,0},{2,1},{3,2},{4,3},{5,4},{6,5},{7,6},{8,7},{9,8},{10,9},{11,1... | collective-permute-start | bytes 1179656 | tf_op jit(solution)/shard_map/ppermute | solution.py:433
  165.6 8.5 %collective-permute-done.low_ref = f32[768,128]{1,0:T(8,128)S(1)} collective-permute-done((f32[768,128]{1,0:T(8,128)S(1)}, f32[768,128]{1,0:T(8,128)S(1)}, u32[]{:S(2)}, u32[]{:S(2)}) %collective-permute-start) | collective-permute-done | bytes 393248 | tf_op jit(solution)/shard_map/ppermute | solution.py:432
  174.0 0.0 copy-start.2
  174.0 0.0 collective-permute-done.1.high_ref
  174.0 0.0 copy-start.3
  174.0 0.0 copy-done
  174.0 0.7 copy-done.2
  174.8 0.1 copy-done.3
  174.9 5.4 %advance.1 = f32[32,3,8,512]{3,2,1,0:T(8,128)} custom-call(f32[3072,128]{1,0:T(8,128)} %bitcast.15, f32[768,128]{1,0:T(8,128)} %copy-done.2, f32[768,128]{1,0:T(8,128)} %copy-done.3), custom_call_target="tpu_custom_call" | custom-call | tf_op jit(solution)/shard_map/advance/pallas_call | solution.py:396
Async XLA Ops:
  46.4 7.2 %copy-start.4 = (s32[1,1,256]{2,1,0:T(1,128)S(1)}, s32[1,1,256]{2,1,0:T(1,128)}, u32[]{:S(2)}) copy-start(s32[1,1,256]{2,1,0:T(1,128)} %param.7) | copy-start | bytes 3076
  46.4 8.0 %copy-start.5 = (f32[1,1,256]{2,1,0:T(1,128)S(1)}, f32[1,1,256]{2,1,0:T(1,128)}, u32[]{:S(2)}) copy-start(f32[1,1,256]{2,1,0:T(1,128)} %param.8) | copy-start | bytes 3076
  46.4 8.8 %copy-start.6 = (f32[1,1,256]{2,1,0:T(1,128)S(1)}, f32[1,1,256]{2,1,0:T(1,128)}, u32[]{:S(2)}) copy-start(f32[1,1,256]{2,1,0:T(1,128)} %param.9) | copy-start | bytes 3076
  46.4 31.6 %all-to-all-start.1 = ((f32[128,1,3072]{2,1,0:T(1,128)}), f32[128,1,3072]{2,1,0:T(1,128)S(1)}, u32[]{:S(2)}, u32[]{:S(2)}) async-start(f32[128,1,3072]{2,1,0:T(1,128)} %bitcast.16), calls=%async_computation.1 | async-start | bytes 3145728 | tf_op jit(solution)/shard_map/all_to_all | solution.py:408
  78.1 1.1 copy-start.1
  160.1 13.9 %copy-start = (f32[8,1,49152]{2,1,0:T(1,128)}, f32[8,1,49152]{2,1,0:T(1,128)S(1)}, u32[]{:S(2)}) copy-start(f32[8,1,49152]{2,1,0:T(1,128)S(1)} %all_to_all.48) | copy-start | bytes 4718596
  160.1 13.9 %collective-permute-start = (f32[768,128]{1,0:T(8,128)S(1)}, f32[768,128]{1,0:T(8,128)S(1)}, u32[]{:S(2)}, u32[]{:S(2)}) collective-permute-start(f32[768,128]{1,0:T(8,128)S(1)} %bitcast.25), channel_id=1, source_target_pairs={{0,1},{1,2},{2,3},{3,4},{4,5},{5,6},{6,7},{7,8},{8,9},{9,10},{10,1... | collective-permute-start | bytes 1179656 | tf_op jit(solution)/shard_map/ppermute | solution.py:432
  160.8 13.2 %collective-permute-start.1 = (f32[768,128]{1,0:T(8,128)S(1)}, f32[768,128]{1,0:T(8,128)S(1)}, u32[]{:S(2)}, u32[]{:S(2)}) collective-permute-start(f32[768,128]{1,0:T(8,128)S(1)} %bitcast.24), channel_id=1, source_target_pairs={{1,0},{2,1},{3,2},{4,3},{5,4},{6,5},{7,6},{8,7},{9,8},{10,9},{11,1... | collective-permute-start | bytes 1179656 | tf_op jit(solution)/shard_map/ppermute | solution.py:433
  174.0 0.7 copy-start.2
  174.0 0.9 copy-start.3

commit v3 on v2

--- a/solution.py
+++ b/solution.py
@@ -24,16 +24,19 @@
 )
 BLOCK = 32
 PANEL = 16
-
-
-def start_kernel(prior_ref, dev_ref, out_ref):
+PIECE = 3
+SPLIT = 2
+
+
+def start_kernel(prior_ref, dev_ref, *out_refs):
     members, fields, rows, width = dev_ref.shape
+    split = len(out_refs)
     for m in range(members):
         for f in range(fields):
             for cb in range(width // LANES):
-                at = ((m * fields + f) * (width // LANES) + cb) * rows
+                at = ((m // split * fields + f) * (width // LANES) + cb) * rows
                 lanes = slice(cb * LANES, (cb + 1) * LANES)
-                out_ref[at : at + rows, :] = dev_ref[m, f, :, lanes] + prior_ref[f, :, lanes]
+                out_refs[m % split][at : at + rows, :] = dev_ref[m, f, :, lanes] + prior_ref[f, :, lanes]
 
 
 def roll_x(field, shift):
@@ -133,7 +136,8 @@
     lax.fori_loop(0, members, member_step, 0)
 
 
-def gram_kernel(in_ref, cell_ref, value_ref, var_ref, pack_ref, dev_ref, mean_ref, *, ensemble, per):
+def gram_kernel(*refs, split, ensemble, per):
+    slabs, (cell_ref, value_ref, var_ref, pack_ref, dev_ref, mean_ref) = refs[:split], refs[split:]
     cells = cell_ref[...]
     inv_var = 1.0 / var_ref[...]
     val_w = value_ref[...] * inv_var
@@ -145,7 +149,7 @@
             hit = cells == lane + j * LANES
             w = jnp.sum(jnp.where(hit, inv_var, 0.0), axis=0, keepdims=True)
             vw = jnp.sum(jnp.where(hit, val_w, 0.0), axis=0, keepdims=True)
-            full = in_ref[pl.ds(j, ensemble, stride=per), :]
+            full = jnp.concatenate([slab[pl.ds(j, ensemble // split, stride=per), :] for slab in slabs], axis=0)
             mean = jnp.sum(full, axis=0, keepdims=True) * (1.0 / ensemble)
             dev = full - mean
             dev_ref[:, j * LANES : (j + 1) * LANES] = dev
@@ -162,24 +166,39 @@
         )
     half = ensemble // 2
     sub = lax.broadcasted_iota(jnp.int32, (half, LANES), 0)
-    for a in range(2):
-        for cb in range(2):
-            pack_ref[pl.ds(a * 2 + cb, half, stride=5), :] = total[
-                a * half : (a + 1) * half, cb * LANES : (cb + 1) * LANES
-            ]
+    col = lax.broadcasted_iota(jnp.int32, (half, LANES), 1)
+    low, high = total[half:ensemble, LANES:], total[:half, :LANES]
+    diagonal = jnp.sum(jnp.where(sub == col, low, 0.0), axis=0, keepdims=True)
     inn = total[ensemble : ensemble + 1, :]
-    pack_ref[pl.ds(4, half, stride=5), :] = jnp.where(
-        sub == 0,
-        jnp.broadcast_to(inn[:, :LANES], (half, LANES)),
-        jnp.where(sub == 1, jnp.broadcast_to(inn[:, LANES:], (half, LANES)), 0.0),
+    pack_ref[pl.ds(0, half, stride=PIECE), :] = total[:half, LANES:]
+    pack_ref[pl.ds(1, half, stride=PIECE), :] = jnp.where(col >= sub, high, low)
+    extra = jnp.zeros((half, LANES), jnp.float32)
+    for i, row in enumerate((inn[:, :LANES], inn[:, LANES:], diagonal)):
+        extra = jnp.where(sub == i, jnp.broadcast_to(row, (half, LANES)), extra)
+    pack_ref[pl.ds(2, half, stride=PIECE), :] = extra
+
+
+def unpack_gram(ref, half):
+    sub = lax.broadcasted_iota(jnp.int32, (half, LANES), 0)
+    col = lax.broadcasted_iota(jnp.int32, (half, LANES), 1)
+    cross = ref[pl.ds(0, half, stride=PIECE), :]
+    both = ref[pl.ds(1, half, stride=PIECE), :]
+    turned = both.T
+    first = jnp.where(col >= sub, both, turned)
+    second = jnp.where(col < sub, both, turned)
+    second = jnp.where(col == sub, jnp.broadcast_to(ref[2 * PIECE + 2 : 2 * PIECE + 3, :], (half, LANES)), second)
+    gram = jnp.concatenate(
+        [jnp.concatenate([first, cross], axis=1), jnp.concatenate([cross.T, second], axis=1)], axis=0
     )
+    innovation = jnp.concatenate([ref[2:3, :], ref[PIECE + 2 : PIECE + 3, :]], axis=1)
+    return gram, innovation
 
 
 def piece_sum_kernel(in_ref, out_ref):
-    count = in_ref.shape[0] // 5
-    for q in range(5):
-        total = jnp.sum(in_ref[pl.ds(q, count, stride=5), :], axis=0, keepdims=True)
-        out_ref[pl.ds(q, count, stride=5), :] = jnp.broadcast_to(total, (count, LANES))
+    count = in_ref.shape[0] // PIECE
+    for q in range(PIECE):
+        total = jnp.sum(in_ref[pl.ds(q, count, stride=PIECE), :], axis=0, keepdims=True)
+        out_ref[pl.ds(q, count, stride=PIECE), :] = jnp.broadcast_to(total, (count, LANES))
 
 
 def split3(x):
@@ -220,19 +239,14 @@
     return jnp.concatenate(rows, axis=0)
 
 
-def root_kernel(in_ref, dev_ref, mean_ref, out_ref, work_ref, *, ensemble, per):
+def root_kernel(in_ref, dev_ref, mean_ref, *refs, ensemble, per):
+    out_refs, work_ref = refs[:-1], refs[-1]
     half = ensemble // 2
     n = ensemble
     row_id = lax.broadcasted_iota(jnp.int32, (n, n), 0)
     lane_id = lax.broadcasted_iota(jnp.int32, (n, n), 1)
     diag = row_id == lane_id
-    gram = jnp.concatenate(
-        [
-            jnp.concatenate([in_ref[pl.ds(a * 2 + cb, half, stride=5), :] for cb in range(2)], axis=1)
-            for a in range(2)
-        ],
-        axis=0,
-    )
+    gram, innovation = unpack_gram(in_ref, half)
     matrix = gram * (1.0 / (ensemble - 1.0))
     for s, shift in enumerate(SHIFT):
         work_ref[s] = matrix + jnp.where(diag, 1.0 + shift, 0.0)
@@ -279,7 +293,6 @@
     root = jnp.where(diag, ROOT_CONST, 0.0)
     for s in range(shifts):
         root = root - ROOT_COEF[s] * work_ref[s]
-    innovation = jnp.concatenate([in_ref[4:5, :], in_ref[9:10, :]], axis=1)
     inner = jnp.sum(root * innovation, axis=1, keepdims=True)
     weights = jnp.sum(root * inner, axis=0, keepdims=True) * (1.0 / (ensemble - 1.0))
     mixing = root + weights
@@ -291,11 +304,15 @@
             precision=lax.Precision.HIGHEST,
             preferred_element_type=jnp.float32,
         ) + mean_ref[0:1, lanes]
-        for i in range(2):
-            out_ref[pl.ds(2 * pair + i, ensemble, stride=per), :] = mixed[:, i * LANES : (i + 1) * LANES]
-
-
-def advance_kernel(main_ref, low_ref, high_ref, out_ref, buf_ref, *, members, per):
+        for part in range(SPLIT):
+            for i in range(2):
+                out_refs[part][pl.ds(2 * pair + i, half, stride=per), :] = mixed[
+                    part * half : (part + 1) * half, i * LANES : (i + 1) * LANES
+                ]
+
+
+def advance_kernel(main_ref, low_ref, high_ref, *refs, members, per):
+    out_ref, buf_ref = refs[-2:]
     blocks = per // 3
     stride = main_ref.shape[0] // 8
     first = pl.program_id(0) * members
@@ -332,9 +349,10 @@
     return jax.ShapeDtypeStruct(shape, jnp.float32)
 
 
-def make_start(prior, deviations):
+def make_start(prior, deviations, split):
     members, fields, rows, width = deviations.shape
     step = 16
+    flat = fields * rows * width // LANES // split
     return pl.pallas_call(
         start_kernel,
         grid=(members // step,),
@@ -342,8 +360,8 @@
             pl.BlockSpec((fields, rows, width), lambda i: (0, 0, 0)),
             pl.BlockSpec((step, fields, rows, width), lambda i: (i, 0, 0, 0)),
         ],
-        out_specs=pl.BlockSpec((step * fields * rows * width // LANES, LANES), lambda i: (i, 0)),
-        out_shape=f32(members * fields * rows * width // LANES, LANES),
+        out_specs=[pl.BlockSpec((step * flat, LANES), lambda i: (i, 0))] * split,
+        out_shape=[f32(members * flat, LANES)] * split,
         name="start",
     )(prior, deviations)
 
@@ -364,14 +382,14 @@
     )(rows)
 
 
-def gram_pieces(rows, cell, value, var, ensemble, per):
-    return pl.pallas_call(
-        functools.partial(gram_kernel, ensemble=ensemble, per=per),
-        in_specs=[VMEM] * 4,
+def gram_pieces(slabs, cell, value, var, ensemble, per):
+    return pl.pallas_call(
+        functools.partial(gram_kernel, split=len(slabs), ensemble=ensemble, per=per),
+        in_specs=[VMEM] * (3 + len(slabs)),
         out_specs=[VMEM] * 3,
-        out_shape=[f32(ensemble // 2 * 5, LANES), f32(ensemble, per * LANES), f32(8, per * LANES)],
+        out_shape=[f32(ensemble // 2 * PIECE, LANES), f32(ensemble, per * LANES), f32(8, per * LANES)],
         name="gram",
-    )(rows, cell, value, var)
+    )(*slabs, cell, value, var)
 
 
 def piece_sum(pieces):
@@ -384,24 +402,26 @@
     return pl.pallas_call(
         functools.partial(root_kernel, ensemble=ensemble, per=per),
         in_specs=[VMEM] * 3,
-        out_specs=VMEM,
-        out_shape=f32(ensemble * per, LANES),
+        out_specs=[VMEM] * SPLIT,
+        out_shape=[f32(ensemble // SPLIT * per, LANES)] * SPLIT,
         scratch_shapes=[pltpu.VMEM((len(SHIFT), ensemble, ensemble), jnp.float32)],
         name="analyse",
     )(pieces, dev, mean)
 
 
-def advance(main, low, high, members, per):
+def advance(main, low, high, earlier, part, split, members, per):
     step = 8
+    width = per // 3 * LANES
     return pl.pallas_call(
         functools.partial(advance_kernel, members=step, per=per),
         grid=(members // step,),
-        in_specs=[VMEM] * 3,
-        out_specs=pl.BlockSpec((step, 3, 8, per // 3 * LANES), lambda i: (i, 0, 0, 0)),
-        out_shape=f32(members, 3, 8, per // 3 * LANES),
+        in_specs=[VMEM] * 3 + [pl.BlockSpec(memory_space=pl.ANY)] * len(earlier),
+        out_specs=pl.BlockSpec((step, None, 3, 8, width), lambda i: (i, part, 0, 0, 0)),
+        out_shape=f32(members, split, 3, 8, width),
         scratch_shapes=[pltpu.VMEM((UNROLL, per // 3 * 4, 24, LANES), jnp.float32)],
+        input_output_aliases={3: 0} if earlier else {},
         name="advance",
-    )(main, low, high)
+    )(main, low, high, *earlier)
 
 
 def exchange(rows, axes, count):
@@ -416,22 +436,28 @@
     per = 3 * blocks
     ensemble = members_dev * runners
     whole = ("runner", "tile")
-    start = make_start(prior_mean_fields, ensemble_deviations)
-    grids = exchange(start, "tile", tiles)
-    forecast = runge_kutta(grids, tiles, members_dev // tiles, blocks)
-    slab = exchange(forecast, whole, runners * tiles)
+    split = members_dev // tiles
+    devices = runners * tiles
+    starts = make_start(prior_mean_fields, ensemble_deviations, split)
+    grids = [exchange(part, "tile", tiles) for part in starts]
+    slabs = [exchange(runge_kutta(part, tiles, 1, blocks), whole, devices) for part in grids]
     pieces, dev, mean = gram_pieces(
-        slab, obs_cell.reshape(-1, 1), obs_value.reshape(-1, 1), obs_var.reshape(-1, 1), ensemble, per
+        slabs, obs_cell.reshape(-1, 1), obs_value.reshape(-1, 1), obs_var.reshape(-1, 1), ensemble, per
     )
-    pieces = exchange(pieces, whole, runners * tiles)
-    pieces = exchange(piece_sum(pieces), whole, runners * tiles)
-    analysed = exchange(analyse(pieces, dev, mean, ensemble, per), "runner", runners)
-    edge = 2 * members_dev * per
+    pieces = exchange(pieces, whole, devices)
+    pieces = exchange(piece_sum(pieces), whole, devices)
+    edge = 2 * tiles * per
     forward = [(i, (i + 1) % tiles) for i in range(tiles)]
     backward = [(target, source) for source, target in forward]
-    low = lax.ppermute(analysed[-edge:], "tile", forward)
-    high = lax.ppermute(analysed[:edge], "tile", backward)
-    return advance(analysed, low, high, members_dev, per)
+    analysed = [exchange(part, "runner", runners) for part in analyse(pieces, dev, mean, ensemble, per)]
+    halos = [
+        (lax.ppermute(part[-edge:], "tile", forward), lax.ppermute(part[:edge], "tile", backward))
+        for part in analysed
+    ]
+    earlier = []
+    for i, (part, halo) in enumerate(zip(analysed, halos)):
+        earlier = [advance(part, *halo, earlier, i, split, tiles, per)]
+    return earlier[0].reshape(ensemble_deviations.shape)
 
 
 def solution(mesh):

time: 181 us -> 188 us (1.039)
  blocking collectives: 89.1 us -> 69.7 us
  starting transfers between devices: 12.6 us -> 29.9 us
  waiting for transfers between devices: 30.5 us -> 35.6 us
  Pallas kernels: 43.5 us -> 46.8 us
    all_to_all x4, blocking collectives: 89.1 us -> 69.7 us  [exchange(): moved = lax.all_to_all(rows.reshape(count, -1), axes, 0, 0, tiled=True)]
    all_to_all x1 -> x4, waiting for transfers between devices: 22 us -> 35.6 us  [exchange(): moved = lax.all_to_all(rows.reshape(count, -1), axes, 0, 0, tiled=True)]
    all_to_all x1 -> x4, starting transfers between devices: 7.17 us -> 19.1 us  [exchange(): moved = lax.all_to_all(rows.reshape(count, -1), axes, 0, 0, tiled=True)]
    ppermute x2 -> x4, waiting for transfers between devices: 8.47 us -> 0.01 us  [the longest x2 0.01 us: per_device(): lax.ppermute(part[:edge], 'tile', backward)]
    ppermute x2 -> x4, starting transfers between devices: 5.41 us -> 10.8 us  [the longest x2 9.53 us: per_device(): lax.ppermute(part[:edge], 'tile', backward)]
    pallas_call x1 -> x2, Pallas kernels: 5.38 us -> 7.07 us  [advance(): pl.pallas_call(functools.partial(advance_kernel, members=step, per=per),...]
    pallas_call x1 -> x2, Pallas kernels: 14.1 us -> 15.6 us  [runge_kutta(): pl.pallas_call(functools.partial(runge_kutta_kernel, tiles=tiles, members...]
  transfers between devices with their start and end apart: 3 -> 8, of which waited for: 2 -> 4; matrix products, arithmetic and copies ran while one was open for 1% -> 1% of each run, Pallas kernels for 0% -> 10%
where the time goes in v3:
time: 188 us; the launch traced here: 187 us
  blocking collectives  69.7 us (37%)
  Pallas kernels  46.8 us (25%)
  waiting for transfers between devices  35.6 us (19%)
  starting transfers between devices  29.9 us (16%)
  local copies, waits for them, and re-layouts  4.93 us (3%)
    all_to_all x4, blocking collectives, exchange(): moved = lax.all_to_all(rows.reshape(count, -1), axes, 0, 0, tiled=True)  69.7 us
    all_to_all x4, waiting for transfers between devices, exchange(): moved = lax.all_to_all(rows.reshape(count, -1), axes, 0, 0, tiled=True)  35.6 us
    all_to_all x4, starting transfers between devices, exchange(): moved = lax.all_to_all(rows.reshape(count, -1), axes, 0, 0, tiled=True)  19.1 us
    pallas_call x1, Pallas kernels, analyse(): pl.pallas_call(functools.partial(root_kernel, ensemble=ensemble, per=per)...  15.7 us
    pallas_call x2, Pallas kernels, runge_kutta(): pl.pallas_call(functools.partial(runge_kutta_kernel, tiles=tiles, members...  15.6 us
    ppermute x2, starting transfers between devices, per_device(): lax.ppermute(part[:edge], 'tile', backward)  9.53 us
    pallas_call x2, Pallas kernels, advance(): pl.pallas_call(functools.partial(advance_kernel, members=step, per=per),...  7.07 us
    pallas_call x1, Pallas kernels, gram_pieces(): pl.pallas_call(functools.partial(gram_kernel, split=len(slabs), ensemble=...  4.39 us
  transfers between devices with their start and end apart: 8, of which 4 were waited for; matrix products, arithmetic and copies ran while one was open for 1% of the time, Pallas kernels for 10%

profile of v3, /device:TPU:0, one launch (start us, length us, event | category | flops | bytes accessed | tf_op | source)
XLA Modules:
  0.0 187.1 jit_solution(14572303532754688131)
XLA Ops:
  0.0 2.3 %start.1 = (f32[1536,128]{1,0:T(8,128)}, f32[1536,128]{1,0:T(8,128)}) custom-call(f32[3,8,512]{2,1,0:T(8,128)} %prior_ref.1, f32[32,3,8,512]{3,2,1,0:T(8,128)} %dev_ref.1), custom_call_target="tpu_custom_call" | custom-call | tf_op jit(solution)/shard_map/start/pallas_call | solution.py:356
  2.3 21.6 %all_to_all.72 = f32[16,1,12288]{2,1,0:T(1,128)} all-to-all(f32[16,1,12288]{2,1,0:T(1,128)} %bitcast.34), channel_id=1, replica_groups=mesh['runner'=8,'tile'=16] {'tile'}, dimensions={0} | all-to-all | bytes 1572864 | tf_op jit(solution)/shard_map/all_to_all | solution.py:428
  23.9 3.6 %all-to-all-start = ((f32[16,1,12288]{2,1,0:T(1,128)}), f32[16,1,12288]{2,1,0:T(1,128)S(1)}, u32[]{:S(2)}, u32[]{:S(2)}) async-start(f32[16,1,12288]{2,1,0:T(1,128)} %bitcast), calls=%async_computation | async-start | bytes 1572864 | tf_op jit(solution)/shard_map/all_to_all | solution.py:428
  27.5 7.8 %runge_kutta.3 = f32[1536,128]{1,0:T(8,128)} custom-call(f32[1536,128]{1,0:T(8,128)} %bitcast.29), custom_call_target="tpu_custom_call" | custom-call | tf_op jit(solution)/shard_map/runge_kutta/pallas_call | solution.py:371
  35.3 5.7 %all-to-all-done = f32[16,1,12288]{2,1,0:T(1,128)S(1)} async-done(((f32[16,1,12288]{2,1,0:T(1,128)}), f32[16,1,12288]{2,1,0:T(1,128)S(1)}, u32[]{:S(2)}, u32[]{:S(2)}) %all-to-all-start) | async-done | bytes 786464 | tf_op jit(solution)/shard_map/all_to_all | solution.py:428
  41.1 7.3 %all-to-all-start.3 = ((f32[128,1,1536]{2,1,0:T(1,128)}), f32[128,1,1536]{2,1,0:T(1,128)S(1)}, u32[]{:S(2)}, u32[]{:S(2)}) async-start(f32[128,1,1536]{2,1,0:T(1,128)} %bitcast.28), calls=%async_computation.3 | async-start | bytes 1572864 | tf_op jit(solution)/shard_map/all_to_all | solution.py:428
  48.4 0.0 copy-done.2
  48.4 0.0 copy-start.9
  48.4 0.0 copy-start.10
  48.4 0.0 copy-start.11
  48.4 7.8 %runge_kutta.2 = f32[1536,128]{1,0:T(8,128)} custom-call(f32[1536,128]{1,0:T(8,128)} %bitcast.26), custom_call_target="tpu_custom_call" | custom-call | tf_op jit(solution)/shard_map/runge_kutta/pallas_call | solution.py:371
  56.3 8.4 %all-to-all-done.3 = f32[128,1,1536]{2,1,0:T(1,128)S(1)} async-done(((f32[128,1,1536]{2,1,0:T(1,128)}), f32[128,1,1536]{2,1,0:T(1,128)S(1)}, u32[]{:S(2)}, u32[]{:S(2)}) %all-to-all-start.3) | async-done | bytes 786464 | tf_op jit(solution)/shard_map/all_to_all | solution.py:428
  64.7 4.6 %all-to-all-start.1 = ((f32[128,1,1536]{2,1,0:T(1,128)}), f32[128,1,1536]{2,1,0:T(1,128)S(1)}, u32[]{:S(2)}, u32[]{:S(2)}) async-start(f32[128,1,1536]{2,1,0:T(1,128)} %bitcast.27), calls=%async_computation.1 | async-start | bytes 1572864 | tf_op jit(solution)/shard_map/all_to_all | solution.py:428
  69.3 0.0 copy-done.9
  69.3 0.8 copy.14.refs_2_
  70.1 0.0 copy-done.10
  70.1 0.8 copy.15.refs_3_
  70.9 0.0 copy-done.11
  70.9 0.8 copy.16.refs_4_
  71.7 13.9 %all-to-all-done.1 = f32[128,1,1536]{2,1,0:T(1,128)S(1)} async-done(((f32[128,1,1536]{2,1,0:T(1,128)}), f32[128,1,1536]{2,1,0:T(1,128)S(1)}, u32[]{:S(2)}, u32[]{:S(2)}) %all-to-all-start.1) | async-done | bytes 786464 | tf_op jit(solution)/shard_map/all_to_all | solution.py:428
  85.6 0.0 copy-done.3
  85.6 0.9 copy-done.4
  86.5 4.4 %gram.1 = (f32[384,128]{1,0:T(8,128)}, f32[256,1536]{1,0:T(8,128)}, f32[8,1536]{1,0:T(8,128)}) custom-call(f32[1536,128]{1,0:T(8,128)} %bitcast.31, f32[1536,128]{1,0:T(8,128)} %bitcast.30, s32[256,1]{1,0:T(8,128)} %copy.14.refs_2_, f32[256,1]{1,0:T(8,128)} %copy.15.refs_3_, f32[256,1]{1,0:T(8,128)} %copy.16.refs_4_), custom_call_target="tpu_custom_call" | custom-call | tf_op jit(solution)/shard_map/gram/pallas_call | solution.py:386
  90.9 15.7 %all_to_all.73 = f32[128,1,384]{2,1,0:T(1,128)} all-to-all(f32[128,1,384]{2,1,0:T(1,128)} %bitcast.37), channel_id=1, replica_groups=mesh['runner'=8,'tile'=16] {'runner','tile'}, dimensions={0} | all-to-all | bytes 393216 | tf_op jit(solution)/shard_map/all_to_all | solution.py:428
  106.7 1.6 piece_sum.1
  108.3 15.7 %all_to_all.74 = f32[128,1,384]{2,1,0:T(1,128)} all-to-all(f32[128,1,384]{2,1,0:T(1,128)} %bitcast.36), channel_id=1, replica_groups=mesh['runner'=8,'tile'=16] {'runner','tile'}, dimensions={0} | all-to-all | bytes 393216 | tf_op jit(solution)/shard_map/all_to_all | solution.py:428
  124.0 15.7 %analyse.1 = (f32[1536,128]{1,0:T(8,128)}, f32[1536,128]{1,0:T(8,128)}) custom-call(f32[384,128]{1,0:T(8,128)} %bitcast.32, f32[256,1536]{1,0:T(8,128)} %get-tuple-element.15.dev_ref, f32[8,1536]{1,0:T(8,128)} %get-tuple-element.16.mean_ref), custom_call_target="tpu_custom_call" | custom-call | tf_op jit(solution)/shard_map/analyse/pallas_call | solution.py:402
  139.7 16.6 %all_to_all.75 = f32[8,1,24576]{2,1,0:T(1,128)S(1)} all-to-all(f32[8,1,24576]{2,1,0:T(1,128)} %bitcast.33), channel_id=1, replica_groups=mesh['runner'=8,'tile'=16] {'runner'}, dimensions={0} | all-to-all | bytes 1572864 | tf_op jit(solution)/shard_map/all_to_all | solution.py:428
  156.4 3.5 %all-to-all-start.6 = ((f32[8,1,24576]{2,1,0:T(1,128)}), f32[8,1,24576]{2,1,0:T(1,128)S(1)}, u32[]{:S(2)}, u32[]{:S(2)}) async-start(f32[8,1,24576]{2,1,0:T(1,128)} %bitcast.15), calls=%async_computation.6 | async-start | bytes 1572864 | tf_op jit(solution)/shard_map/all_to_all | solution.py:428
  160.0 0.7 collective-permute-start.2
  160.6 4.8 %collective-permute-start.3 = (f32[384,128]{1,0:T(8,128)S(1)}, f32[384,128]{1,0:T(8,128)S(1)}, u32[]{:S(2)}, u32[]{:S(2)}) collective-permute-start(f32[384,128]{1,0:T(8,128)S(1)} %bitcast.38), channel_id=1, source_target_pairs={{1,0},{2,1},{3,2},{4,3},{5,4},{6,5},{7,6},{8,7},{9,8},{10,9},{11,1... | collective-permute-start | bytes 589832 | tf_op jit(solution)/shard_map/ppermute | solution.py:454
  165.4 7.6 %all-to-all-done.6 = f32[8,1,24576]{2,1,0:T(1,128)S(1)} async-done(((f32[8,1,24576]{2,1,0:T(1,128)}), f32[8,1,24576]{2,1,0:T(1,128)S(1)}, u32[]{:S(2)}, u32[]{:S(2)}) %all-to-all-start.6) | async-done | bytes 786464 | tf_op jit(solution)/shard_map/all_to_all | solution.py:428
  173.0 0.0 copy-done
  173.0 0.7 collective-permute-start
  173.7 4.8 %collective-permute-start.1 = (f32[384,128]{1,0:T(8,128)S(1)}, f32[384,128]{1,0:T(8,128)S(1)}, u32[]{:S(2)}, u32[]{:S(2)}) collective-permute-start(f32[384,128]{1,0:T(8,128)S(1)} %bitcast.40), channel_id=1, source_target_pairs={{1,0},{2,1},{3,2},{4,3},{5,4},{6,5},{7,6},{8,7},{9,8},{10,9},{11,1... | collective-permute-start | bytes 589832 | tf_op jit(solution)/shard_map/ppermute | solution.py:454
  178.4 0.0 collective-permute-done.2.low_ref
  178.4 0.0 collective-permute-done.3.high_ref
  178.4 0.0 copy-start.8
  178.4 0.7 copy-done.7
  179.1 0.1 copy-done.8
  179.2 3.5 %advance.2.refs_0_ = f32[16,2,3,8,512]{4,3,2,1,0:T(8,128)} custom-call(f32[1536,128]{1,0:T(8,128)} %bitcast.24, f32[384,128]{1,0:T(8,128)} %copy-done.7, f32[384,128]{1,0:T(8,128)} %copy-done.8), custom_call_target="tpu_custom_call" | custom-call | tf_op jit(solution)/shard_map/advance/pallas_call | solution.py:415
  182.8 0.0 copy-done.1
  182.8 0.0 collective-permute-done.low_ref
  182.8 0.0 collective-permute-done.1.high_ref
  182.8 0.0 copy-start.6
  182.8 0.7 copy-done.5
  183.4 0.1 copy-done.6
  183.5 3.5 %advance.3 = f32[16,2,3,8,512]{4,3,2,1,0:T(8,128)} custom-call(f32[1536,128]{1,0:T(8,128)} %bitcast.25, f32[384,128]{1,0:T(8,128)} %copy-done.5, f32[384,128]{1,0:T(8,128)} %copy-done.6, f32[16,2,3,8,512]{4,3,2,1,0:T(8,128)} %advance.2.refs_0_), custom_call_target="tpu_custom_call", output_to_operand_aliasing={{}: (3, {})} | custom-call | tf_op jit(solution)/shard_map/advance/pallas_call | solution.py:415
  (9 shorter events, 0.1 us)
Async XLA Ops:
  23.9 17.2 %all-to-all-start = ((f32[16,1,12288]{2,1,0:T(1,128)}), f32[16,1,12288]{2,1,0:T(1,128)S(1)}, u32[]{:S(2)}, u32[]{:S(2)}) async-start(f32[16,1,12288]{2,1,0:T(1,128)} %bitcast), calls=%async_computation | async-start | bytes 1572864 | tf_op jit(solution)/shard_map/all_to_all | solution.py:428
  41.1 7.3 %copy-start.2 = (f32[16,1,12288]{2,1,0:T(1,128)}, f32[16,1,12288]{2,1,0:T(1,128)S(1)}, u32[]{:S(2)}) copy-start(f32[16,1,12288]{2,1,0:T(1,128)S(1)} %all-to-all-done) | copy-start | bytes 2359300
  41.1 23.6 %all-to-all-start.3 = ((f32[128,1,1536]{2,1,0:T(1,128)}), f32[128,1,1536]{2,1,0:T(1,128)S(1)}, u32[]{:S(2)}, u32[]{:S(2)}) async-start(f32[128,1,1536]{2,1,0:T(1,128)} %bitcast.28), calls=%async_computation.3 | async-start | bytes 1572864 | tf_op jit(solution)/shard_map/all_to_all | solution.py:428
  48.4 20.9 %copy-start.9 = (s32[1,1,256]{2,1,0:T(1,128)S(1)}, s32[1,1,256]{2,1,0:T(1,128)}, u32[]{:S(2)}) copy-start(s32[1,1,256]{2,1,0:T(1,128)} %param.7) | copy-start | bytes 3076
  48.4 21.7 %copy-start.10 = (f32[1,1,256]{2,1,0:T(1,128)S(1)}, f32[1,1,256]{2,1,0:T(1,128)}, u32[]{:S(2)}) copy-start(f32[1,1,256]{2,1,0:T(1,128)} %param.8) | copy-start | bytes 3076
  48.4 22.5 %copy-start.11 = (f32[1,1,256]{2,1,0:T(1,128)S(1)}, f32[1,1,256]{2,1,0:T(1,128)}, u32[]{:S(2)}) copy-start(f32[1,1,256]{2,1,0:T(1,128)} %param.9) | copy-start | bytes 3076
  64.7 20.9 %copy-start.3 = (f32[128,1,1536]{2,1,0:T(1,128)}, f32[128,1,1536]{2,1,0:T(1,128)S(1)}, u32[]{:S(2)}) copy-start(f32[128,1,1536]{2,1,0:T(1,128)S(1)} %all-to-all-done.3) | copy-start | bytes 2359300
  64.7 20.9 %all-to-all-start.1 = ((f32[128,1,1536]{2,1,0:T(1,128)}), f32[128,1,1536]{2,1,0:T(1,128)S(1)}, u32[]{:S(2)}, u32[]{:S(2)}) async-start(f32[128,1,1536]{2,1,0:T(1,128)} %bitcast.27), calls=%async_computation.1 | async-start | bytes 1572864 | tf_op jit(solution)/shard_map/all_to_all | solution.py:428
  85.6 0.9 copy-start.4
  156.4 16.6 %copy-start = (f32[8,1,24576]{2,1,0:T(1,128)}, f32[8,1,24576]{2,1,0:T(1,128)S(1)}, u32[]{:S(2)}) copy-start(f32[8,1,24576]{2,1,0:T(1,128)S(1)} %all_to_all.75) | copy-start | bytes 2359300
  156.4 16.6 %all-to-all-start.6 = ((f32[8,1,24576]{2,1,0:T(1,128)}), f32[8,1,24576]{2,1,0:T(1,128)S(1)}, u32[]{:S(2)}, u32[]{:S(2)}) async-start(f32[8,1,24576]{2,1,0:T(1,128)} %bitcast.15), calls=%async_computation.6 | async-start | bytes 1572864 | tf_op jit(solution)/shard_map/all_to_all | solution.py:428
  160.0 18.5 %collective-permute-start.2 = (f32[384,128]{1,0:T(8,128)S(1)}, f32[384,128]{1,0:T(8,128)S(1)}, u32[]{:S(2)}, u32[]{:S(2)}) collective-permute-start(f32[384,128]{1,0:T(8,128)S(1)} %bitcast.39), channel_id=1, source_target_pairs={{0,1},{1,2},{2,3},{3,4},{4,5},{5,6},{6,7},{7,8},{8,9},{9,10},{10,1... | collective-permute-start | bytes 589832 | tf_op jit(solution)/shard_map/ppermute | solution.py:454
  160.6 17.8 %collective-permute-start.3 = (f32[384,128]{1,0:T(8,128)S(1)}, f32[384,128]{1,0:T(8,128)S(1)}, u32[]{:S(2)}, u32[]{:S(2)}) collective-permute-start(f32[384,128]{1,0:T(8,128)S(1)} %bitcast.38), channel_id=1, source_target_pairs={{1,0},{2,1},{3,2},{4,3},{5,4},{6,5},{7,6},{8,7},{9,8},{10,9},{11,1... | collective-permute-start | bytes 589832 | tf_op jit(solution)/shard_map/ppermute | solution.py:454
  173.0 9.8 %copy-start.1 = (f32[8,1,24576]{2,1,0:T(1,128)}, f32[8,1,24576]{2,1,0:T(1,128)S(1)}, u32[]{:S(2)}) copy-start(f32[8,1,24576]{2,1,0:T(1,128)S(1)} %all-to-all-done.6) | copy-start | bytes 2359300
  173.0 9.7 %collective-permute-start = (f32[384,128]{1,0:T(8,128)S(1)}, f32[384,128]{1,0:T(8,128)S(1)}, u32[]{:S(2)}, u32[]{:S(2)}) collective-permute-start(f32[384,128]{1,0:T(8,128)S(1)} %bitcast.41), channel_id=1, source_target_pairs={{0,1},{1,2},{2,3},{3,4},{4,5},{5,6},{6,7},{7,8},{8,9},{9,10},{10,1... | collective-permute-start | bytes 589832 | tf_op jit(solution)/shard_map/ppermute | solution.py:454
  173.7 9.1 %collective-permute-start.1 = (f32[384,128]{1,0:T(8,128)S(1)}, f32[384,128]{1,0:T(8,128)S(1)}, u32[]{:S(2)}, u32[]{:S(2)}) collective-permute-start(f32[384,128]{1,0:T(8,128)S(1)} %bitcast.40), channel_id=1, source_target_pairs={{1,0},{2,1},{3,2},{4,3},{5,4},{6,5},{7,6},{8,7},{9,8},{10,9},{11,1... | collective-permute-start | bytes 589832 | tf_op jit(solution)/shard_map/ppermute | solution.py:454
  178.4 0.7 copy-start.7
  178.4 0.8 copy-start.8
  182.8 0.7 copy-start.5
  182.8 0.7 copy-start.6

commit v4 on v2

--- a/solution.py
+++ b/solution.py
@@ -24,6 +24,7 @@
 )
 BLOCK = 32
 PANEL = 16
+PIECE = 3
 
 
 def start_kernel(prior_ref, dev_ref, out_ref):
@@ -133,11 +134,21 @@
     lax.fori_loop(0, members, member_step, 0)
 
 
-def gram_kernel(in_ref, cell_ref, value_ref, var_ref, pack_ref, dev_ref, mean_ref, *, ensemble, per):
-    cells = cell_ref[...]
-    inv_var = 1.0 / var_ref[...]
-    val_w = value_ref[...] * inv_var
-    lane = lax.broadcasted_iota(jnp.int32, (cells.shape[0], LANES), 1)
+def gram_kernel(
+    in_ref, cell_ref, value_ref, var_ref, pack_ref, dev_ref, mean_ref, buf_ref, sem_ref, *, ensemble, per
+):
+    inverse = 1.0 / var_ref[...]
+    count = inverse.shape[1]
+    observed = jnp.concatenate(
+        [cell_ref[...].astype(jnp.float32), inverse, value_ref[...] * inverse, jnp.zeros((5, count), jnp.float32)],
+        axis=0,
+    ).T
+    cells, inv_var, val_w = (
+        jnp.broadcast_to(observed[:, i : i + 1], (count, LANES)) for i in range(3)
+    )
+    cells = cells.astype(jnp.int32)
+    copies = []
+    lane = lax.broadcasted_iota(jnp.int32, (count, LANES), 1)
     total = jnp.zeros((ensemble + 8, ensemble), jnp.float32)
     for pair in range(per // 2):
         devs, lefts = [], []
@@ -148,11 +159,14 @@
             full = in_ref[pl.ds(j, ensemble, stride=per), :]
             mean = jnp.sum(full, axis=0, keepdims=True) * (1.0 / ensemble)
             dev = full - mean
-            dev_ref[:, j * LANES : (j + 1) * LANES] = dev
+            buf_ref[:, j * LANES : (j + 1) * LANES] = dev
             mean_ref[:, j * LANES : (j + 1) * LANES] = jnp.broadcast_to(mean, (8, LANES))
             devs.append(dev)
             z = jnp.broadcast_to(vw - mean * w, (8, LANES))
             lefts.append(jnp.concatenate([dev * w, z], axis=0))
+        lanes = slice(pair * 2 * LANES, (pair + 1) * 2 * LANES)
+        copies.append(pltpu.make_async_copy(buf_ref.at[:, lanes], dev_ref.at[:, lanes], sem_ref.at[pair]))
+        copies[-1].start()
         total = total + lax.dot_general(
             jnp.concatenate(lefts, axis=1),
             jnp.concatenate(devs, axis=1),
@@ -162,24 +176,41 @@
         )
     half = ensemble // 2
     sub = lax.broadcasted_iota(jnp.int32, (half, LANES), 0)
-    for a in range(2):
-        for cb in range(2):
-            pack_ref[pl.ds(a * 2 + cb, half, stride=5), :] = total[
-                a * half : (a + 1) * half, cb * LANES : (cb + 1) * LANES
-            ]
+    col = lax.broadcasted_iota(jnp.int32, (half, LANES), 1)
+    low, high = total[half:ensemble, LANES:], total[:half, :LANES]
+    diagonal = jnp.sum(jnp.where(sub == col, low, 0.0), axis=0, keepdims=True)
     inn = total[ensemble : ensemble + 1, :]
-    pack_ref[pl.ds(4, half, stride=5), :] = jnp.where(
-        sub == 0,
-        jnp.broadcast_to(inn[:, :LANES], (half, LANES)),
-        jnp.where(sub == 1, jnp.broadcast_to(inn[:, LANES:], (half, LANES)), 0.0),
+    pack_ref[pl.ds(0, half, stride=PIECE), :] = total[:half, LANES:]
+    pack_ref[pl.ds(1, half, stride=PIECE), :] = jnp.where(col >= sub, high, low)
+    extra = jnp.zeros((half, LANES), jnp.float32)
+    for i, row in enumerate((inn[:, :LANES], inn[:, LANES:], diagonal)):
+        extra = jnp.where(sub == i, jnp.broadcast_to(row, (half, LANES)), extra)
+    pack_ref[pl.ds(2, half, stride=PIECE), :] = extra
+    for copy in copies:
+        copy.wait()
+
+
+def unpack_gram(ref, half):
+    sub = lax.broadcasted_iota(jnp.int32, (half, LANES), 0)
+    col = lax.broadcasted_iota(jnp.int32, (half, LANES), 1)
+    cross = ref[pl.ds(0, half, stride=PIECE), :]
+    both = ref[pl.ds(1, half, stride=PIECE), :]
+    turned = both.T
+    first = jnp.where(col >= sub, both, turned)
+    second = jnp.where(col < sub, both, turned)
+    second = jnp.where(col == sub, jnp.broadcast_to(ref[2 * PIECE + 2 : 2 * PIECE + 3, :], (half, LANES)), second)
+    gram = jnp.concatenate(
+        [jnp.concatenate([first, cross], axis=1), jnp.concatenate([cross.T, second], axis=1)], axis=0
     )
+    innovation = jnp.concatenate([ref[2:3, :], ref[PIECE + 2 : PIECE + 3, :]], axis=1)
+    return gram, innovation
 
 
 def piece_sum_kernel(in_ref, out_ref):
-    count = in_ref.shape[0] // 5
-    for q in range(5):
-        total = jnp.sum(in_ref[pl.ds(q, count, stride=5), :], axis=0, keepdims=True)
-        out_ref[pl.ds(q, count, stride=5), :] = jnp.broadcast_to(total, (count, LANES))
+    count = in_ref.shape[0] // PIECE
+    for q in range(PIECE):
+        total = jnp.sum(in_ref[pl.ds(q, count, stride=PIECE), :], axis=0, keepdims=True)
+        out_ref[pl.ds(q, count, stride=PIECE), :] = jnp.broadcast_to(total, (count, LANES))
 
 
 def split3(x):
@@ -220,19 +251,15 @@
     return jnp.concatenate(rows, axis=0)
 
 
-def root_kernel(in_ref, dev_ref, mean_ref, out_ref, work_ref, *, ensemble, per):
+def root_kernel(in_ref, dev_ref, mean_ref, out_ref, work_ref, buf_ref, sem_ref, *, ensemble, per):
+    fetch = pltpu.make_async_copy(dev_ref, buf_ref, sem_ref)
+    fetch.start()
     half = ensemble // 2
     n = ensemble
     row_id = lax.broadcasted_iota(jnp.int32, (n, n), 0)
     lane_id = lax.broadcasted_iota(jnp.int32, (n, n), 1)
     diag = row_id == lane_id
-    gram = jnp.concatenate(
-        [
-            jnp.concatenate([in_ref[pl.ds(a * 2 + cb, half, stride=5), :] for cb in range(2)], axis=1)
-            for a in range(2)
-        ],
-        axis=0,
-    )
+    gram, innovation = unpack_gram(in_ref, half)
     matrix = gram * (1.0 / (ensemble - 1.0))
     for s, shift in enumerate(SHIFT):
         work_ref[s] = matrix + jnp.where(diag, 1.0 + shift, 0.0)
@@ -279,15 +306,15 @@
     root = jnp.where(diag, ROOT_CONST, 0.0)
     for s in range(shifts):
         root = root - ROOT_COEF[s] * work_ref[s]
-    innovation = jnp.concatenate([in_ref[4:5, :], in_ref[9:10, :]], axis=1)
     inner = jnp.sum(root * innovation, axis=1, keepdims=True)
     weights = jnp.sum(root * inner, axis=0, keepdims=True) * (1.0 / (ensemble - 1.0))
     mixing = root + weights
+    fetch.wait()
     for pair in range(per // 2):
         lanes = slice(pair * 2 * LANES, (pair + 1) * 2 * LANES)
         mixed = jnp.dot(
             mixing,
-            dev_ref[:, lanes],
+            buf_ref[:, lanes],
             precision=lax.Precision.HIGHEST,
             preferred_element_type=jnp.float32,
         ) + mean_ref[0:1, lanes]
@@ -297,13 +324,18 @@
 
 def advance_kernel(main_ref, low_ref, high_ref, out_ref, buf_ref, *, members, per):
     blocks = per // 3
-    stride = main_ref.shape[0] // 8
+    here = main_ref.reshape(8 * members * per, LANES)
+    stride = low_ref.shape[0] // 2
     first = pl.program_id(0) * members
 
     def one(i, slot):
         m = first + i
-        for at, ref, count in ((6, low_ref, 2), (8, main_ref, 8), (16, high_ref, 2)):
-            parts = [ref[pl.ds(m * per + j, count, stride=stride), :] for j in range(per)]
+        for at, ref, count, row, apart in (
+            (6, low_ref, 2, m * per, stride),
+            (8, here, 8, i * per, members * per),
+            (16, high_ref, 2, m * per, stride),
+        ):
+            parts = [ref[pl.ds(row + j, count, stride=apart), :] for j in range(per)]
             parts += [(1.0 + parts[cb]) * parts[2 * blocks + cb] for cb in range(blocks)]
             for j, part in enumerate(parts):
                 buf_ref[slot, j, at : at + count, :] = part
@@ -326,10 +358,19 @@
 
 
 VMEM = pl.BlockSpec(memory_space=pltpu.VMEM)
+HBM = pl.BlockSpec(memory_space=pl.ANY)
 
 
 def f32(*shape):
     return jax.ShapeDtypeStruct(shape, jnp.float32)
+
+
+def near(*shape):
+    return pltpu.VMEM(shape, jnp.float32)
+
+
+def in_vmem(x):
+    return pltpu.with_memory_space_constraint(x, pltpu.VMEM)
 
 
 def make_start(prior, deviations):
@@ -343,7 +384,7 @@
             pl.BlockSpec((step, fields, rows, width), lambda i: (i, 0, 0, 0)),
         ],
         out_specs=pl.BlockSpec((step * fields * rows * width // LANES, LANES), lambda i: (i, 0)),
-        out_shape=f32(members * fields * rows * width // LANES, LANES),
+        out_shape=near(members * fields * rows * width // LANES, LANES),
         name="start",
     )(prior, deviations)
 
@@ -354,41 +395,49 @@
         functools.partial(runge_kutta_kernel, tiles=tiles, members=members, blocks=blocks),
         in_specs=[VMEM],
         out_specs=VMEM,
-        out_shape=f32(*rows.shape),
+        out_shape=near(*rows.shape),
         scratch_shapes=[
             pltpu.VMEM((4 * blocks, tiles * 8 + 16, LANES), jnp.float32),
             pltpu.VMEM((4 * blocks, tiles * 8 + 16, LANES), jnp.float32),
             pltpu.VMEM((3, tiles * 8, blocks * LANES), jnp.float32),
         ],
         name="runge_kutta",
-    )(rows)
+    )(in_vmem(rows))
 
 
 def gram_pieces(rows, cell, value, var, ensemble, per):
     return pl.pallas_call(
         functools.partial(gram_kernel, ensemble=ensemble, per=per),
         in_specs=[VMEM] * 4,
-        out_specs=[VMEM] * 3,
-        out_shape=[f32(ensemble // 2 * 5, LANES), f32(ensemble, per * LANES), f32(8, per * LANES)],
+        out_specs=[VMEM, HBM, VMEM],
+        out_shape=[near(ensemble // 2 * PIECE, LANES), f32(ensemble, per * LANES), near(8, per * LANES)],
+        scratch_shapes=[
+            pltpu.VMEM((ensemble, per * LANES), jnp.float32),
+            pltpu.SemaphoreType.DMA((per // 2,)),
+        ],
         name="gram",
-    )(rows, cell, value, var)
+    )(in_vmem(rows), cell, value, var)
 
 
 def piece_sum(pieces):
     return pl.pallas_call(
-        piece_sum_kernel, in_specs=[VMEM], out_specs=VMEM, out_shape=f32(*pieces.shape), name="piece_sum"
-    )(pieces)
+        piece_sum_kernel, in_specs=[VMEM], out_specs=VMEM, out_shape=near(*pieces.shape), name="piece_sum"
+    )(in_vmem(pieces))
 
 
 def analyse(pieces, dev, mean, ensemble, per):
     return pl.pallas_call(
         functools.partial(root_kernel, ensemble=ensemble, per=per),
-        in_specs=[VMEM] * 3,
+        in_specs=[VMEM, HBM, VMEM],
         out_specs=VMEM,
-        out_shape=f32(ensemble * per, LANES),
-        scratch_shapes=[pltpu.VMEM((len(SHIFT), ensemble, ensemble), jnp.float32)],
+        out_shape=near(ensemble * per, LANES),
+        scratch_shapes=[
+            pltpu.VMEM((len(SHIFT), ensemble, ensemble), jnp.float32),
+            pltpu.VMEM((ensemble, per * LANES), jnp.float32),
+            pltpu.SemaphoreType.DMA(()),
+        ],
         name="analyse",
-    )(pieces, dev, mean)
+    )(in_vmem(pieces), dev, in_vmem(mean))
 
 
 def advance(main, low, high, members, per):
@@ -396,12 +445,12 @@
     return pl.pallas_call(
         functools.partial(advance_kernel, members=step, per=per),
         grid=(members // step,),
-        in_specs=[VMEM] * 3,
+        in_specs=[pl.BlockSpec((8, step * per, LANES), lambda i: (0, i, 0)), VMEM, VMEM],
         out_specs=pl.BlockSpec((step, 3, 8, per // 3 * LANES), lambda i: (i, 0, 0, 0)),
         out_shape=f32(members, 3, 8, per // 3 * LANES),
         scratch_shapes=[pltpu.VMEM((UNROLL, per // 3 * 4, 24, LANES), jnp.float32)],
         name="advance",
-    )(main, low, high)
+    )(main.reshape(8, members * per, LANES), in_vmem(low), in_vmem(high))
 
 
 def exchange(rows, axes, count):
@@ -421,7 +470,7 @@
     forecast = runge_kutta(grids, tiles, members_dev // tiles, blocks)
     slab = exchange(forecast, whole, runners * tiles)
     pieces, dev, mean = gram_pieces(
-        slab, obs_cell.reshape(-1, 1), obs_value.reshape(-1, 1), obs_var.reshape(-1, 1), ensemble, per
+        slab, obs_cell[0], obs_value[0], obs_var[0], ensemble, per
     )
     pieces = exchange(pieces, whole, runners * tiles)
     pieces = exchange(piece_sum(pieces), whole, runners * tiles)

time: 181 us -> 165 us (0.912)
  blocking collectives: 89.1 us -> 114 us
  waiting for transfers between devices: 30.5 us -> 8.47 us
  starting transfers between devices: 12.6 us -> 5.41 us
  Pallas kernels: 43.5 us -> 36.8 us
  local copies, waits for them, and re-layouts: 4.48 us -> 0.06 us
    all_to_all x4 -> x5, blocking collectives: 89.1 us -> 114 us  [exchange(): moved = lax.all_to_all(rows.reshape(count, -1), axes, 0, 0, tiled=True)]
    all_to_all x1 -> x0, waiting for transfers between devices: 22 us -> none  [exchange(): moved = lax.all_to_all(rows.reshape(count, -1), axes, 0, 0, tiled=True)]
    all_to_all x1 -> x0, starting transfers between devices: 7.17 us -> none  [exchange(): moved = lax.all_to_all(rows.reshape(count, -1), axes, 0, 0, tiled=True)]
    pallas_call x1, Pallas kernels: 14.1 us -> 11.5 us  [runge_kutta(): pl.pallas_call(functools.partial(runge_kutta_kernel, tiles=tiles, members...]
    reshape x3 -> x0, local copies, waits for them, and re-layouts: 2.41 us -> none  [the longest x1 0.81 us: per_device(): obs_cell.reshape(-1, 1)]
    unnamed x14 -> x2, local copies, waits for them, and re-layouts: 2.03 us -> 0.01 us
  transfers between devices with their start and end apart: 3 -> 2, of which waited for: 2 -> 1; matrix products, arithmetic and copies ran while one was open for 1% -> 0% of each run, Pallas kernels for 0% -> 0%
where the time goes in v4:
time: 165 us
  blocking collectives  114 us (69%)
  Pallas kernels  36.8 us (22%)
  waiting for transfers between devices  8.47 us (5%)
  starting transfers between devices  5.41 us (3%)
    all_to_all x5, blocking collectives, exchange(): moved = lax.all_to_all(rows.reshape(count, -1), axes, 0, 0, tiled=True)  114 us
    pallas_call x1, Pallas kernels, analyse(): pl.pallas_call(functools.partial(root_kernel, ensemble=ensemble, per=per)...  14.4 us
    pallas_call x1, Pallas kernels, runge_kutta(): pl.pallas_call(functools.partial(runge_kutta_kernel, tiles=tiles, members...  11.5 us
    ppermute x1, waiting for transfers between devices, per_device(): low = lax.ppermute(analysed[-edge:], 'tile', forward)  8.46 us
    pallas_call x1, Pallas kernels, advance(): pl.pallas_call(functools.partial(advance_kernel, members=step, per=per),...  5.23 us
    ppermute x1, starting transfers between devices, per_device(): high = lax.ppermute(analysed[:edge], 'tile', backward)  4.76 us
    pallas_call x1, Pallas kernels, gram_pieces(): pl.pallas_call(functools.partial(gram_kernel, ensemble=ensemble, per=per)...  4.19 us
  transfers between devices with their start and end apart: 2, of which 1 were waited for; matrix products, arithmetic and copies ran while one was open for 0% of the time, Pallas kernels for 0%

profile of v4, /device:TPU:0, one launch (start us, length us, event | category | flops | bytes accessed | tf_op | source)
XLA Modules:
  0.0 165.0 jit_solution(16558411995608773955)
XLA Ops:
  0.0 1.5 start.1
  1.5 29.7 %all_to_all.45 = f32[16,1,24576]{2,1,0:T(1,128)S(1)} all-to-all(f32[16,1,24576]{2,1,0:T(1,128)S(1)} %bitcast.19), channel_id=1, replica_groups=mesh['runner'=8,'tile'=16] {'tile'}, dimensions={0} | all-to-all | bytes 3145728 | tf_op jit(solution)/shard_map/all_to_all | solution.py:457
  31.2 11.5 %runge_kutta.1 = f32[3072,128]{1,0:T(8,128)S(1)} custom-call(f32[3072,128]{1,0:T(8,128)S(1)} %bitcast.17), custom_call_target="tpu_custom_call" | custom-call | tf_op jit(solution)/shard_map/runge_kutta/pallas_call | solution.py:394
  42.7 31.4 %all_to_all.46 = f32[128,1,3072]{2,1,0:T(1,128)S(1)} all-to-all(f32[128,1,3072]{2,1,0:T(1,128)S(1)} %bitcast.18), channel_id=1, replica_groups=mesh['runner'=8,'tile'=16] {'runner','tile'}, dimensions={0} | all-to-all | bytes 3145728 | tf_op jit(solution)/shard_map/all_to_all | solution.py:457
  74.1 4.2 %gram.1 = (f32[384,128]{1,0:T(8,128)S(1)}, f32[256,1536]{1,0:T(8,128)}, f32[8,1536]{1,0:T(8,128)S(1)}) custom-call(f32[3072,128]{1,0:T(8,128)S(1)} %bitcast.15, s32[1,256]{1,0:T(1,128)} %bitcast.27, f32[1,256]{1,0:T(1,128)} %bitcast.28, f32[1,256]{1,0:T(1,128)} %bitcast.29), custom_call_target="tpu_custom_call" | custom-call | tf_op jit(solution)/shard_map/gram/pallas_call | solution.py:409
  78.3 14.4 %all_to_all.47 = f32[128,1,384]{2,1,0:T(1,128)S(1)} all-to-all(f32[128,1,384]{2,1,0:T(1,128)S(1)} %bitcast.23), channel_id=1, replica_groups=mesh['runner'=8,'tile'=16] {'runner','tile'}, dimensions={0} | all-to-all | bytes 393216 | tf_op jit(solution)/shard_map/all_to_all | solution.py:457
  92.8 14.6 %all_to_all.48 = f32[128,1,384]{2,1,0:T(1,128)S(1)} all-to-all(f32[128,1,384]{2,1,0:T(1,128)S(1)} %bitcast.22), channel_id=1, replica_groups=mesh['runner'=8,'tile'=16] {'runner','tile'}, dimensions={0} | all-to-all | bytes 393216 | tf_op jit(solution)/shard_map/all_to_all | solution.py:457
  107.4 14.4 %analyse.1 = f32[3072,128]{1,0:T(8,128)S(1)} custom-call(f32[384,128]{1,0:T(8,128)S(1)} %bitcast.20, f32[256,1536]{1,0:T(8,128)} %get-tuple-element.9.dev_ref, f32[8,1536]{1,0:T(8,128)S(1)} %get-tuple-element.10.mean_ref), custom_call_target="tpu_custom_call" | custom-call | tf_op jit(solution)/shard_map/analyse/pallas_call | solution.py:429
  121.8 24.0 %all_to_all.49 = f32[8,1,49152]{2,1,0:T(1,128)S(1)} all-to-all(f32[8,1,49152]{2,1,0:T(1,128)S(1)} %bitcast.16), channel_id=1, replica_groups=mesh['runner'=8,'tile'=16] {'runner'}, dimensions={0} | all-to-all | bytes 3145728 | tf_op jit(solution)/shard_map/all_to_all | solution.py:457
  145.8 0.0 copy-start
  145.8 0.1 fusion
  145.8 0.7 collective-permute-start
  146.5 4.8 %collective-permute-start.1 = (f32[768,128]{1,0:T(8,128)S(1)}, f32[768,128]{1,0:T(8,128)S(1)}, u32[]{:S(2)}, u32[]{:S(2)}) collective-permute-start(f32[768,128]{1,0:T(8,128)S(1)} %bitcast.25), channel_id=1, source_target_pairs={{1,0},{2,1},{3,2},{4,3},{5,4},{6,5},{7,6},{8,7},{9,8},{10,9},{11,1... | collective-permute-start | bytes 1179656 | tf_op jit(solution)/shard_map/ppermute | solution.py:482
  151.3 8.5 %collective-permute-done.low_ref = f32[768,128]{1,0:T(8,128)S(1)} collective-permute-done((f32[768,128]{1,0:T(8,128)S(1)}, f32[768,128]{1,0:T(8,128)S(1)}, u32[]{:S(2)}, u32[]{:S(2)}) %collective-permute-start) | collective-permute-done | bytes 393248 | tf_op jit(solution)/shard_map/ppermute | solution.py:481
  159.7 0.0 collective-permute-done.1.high_ref
  159.7 0.0 copy-done
  159.7 5.2 %advance.1 = f32[32,3,8,512]{3,2,1,0:T(8,128)} custom-call(f32[8,384,128]{2,1,0:T(8,128)} %bitcast.24, f32[768,128]{1,0:T(8,128)S(1)} %collective-permute-done.low_ref, f32[768,128]{1,0:T(8,128)S(1)} %collective-permute-done.1.high_ref), custom_call_target="tpu_custom_call" | custom-call | tf_op jit(solution)/shard_map/advance/pallas_call | solution.py:445
  (1 shorter events, 0.0 us)
Async XLA Ops:
  145.8 13.9 %copy-start = (f32[8,1,49152]{2,1,0:T(1,128)}, f32[8,1,49152]{2,1,0:T(1,128)S(1)}, u32[]{:S(2)}) copy-start(f32[8,1,49152]{2,1,0:T(1,128)S(1)} %all_to_all.49) | copy-start | bytes 4718596
  145.8 13.9 %collective-permute-start = (f32[768,128]{1,0:T(8,128)S(1)}, f32[768,128]{1,0:T(8,128)S(1)}, u32[]{:S(2)}, u32[]{:S(2)}) collective-permute-start(f32[768,128]{1,0:T(8,128)S(1)} %bitcast.26), channel_id=1, source_target_pairs={{0,1},{1,2},{2,3},{3,4},{4,5},{5,6},{6,7},{7,8},{8,9},{9,10},{10,1... | collective-permute-start | bytes 1179656 | tf_op jit(solution)/shard_map/ppermute | solution.py:481
  146.5 13.2 %collective-permute-start.1 = (f32[768,128]{1,0:T(8,128)S(1)}, f32[768,128]{1,0:T(8,128)S(1)}, u32[]{:S(2)}, u32[]{:S(2)}) collective-permute-start(f32[768,128]{1,0:T(8,128)S(1)} %bitcast.25), channel_id=1, source_target_pairs={{1,0},{2,1},{3,2},{4,3},{5,4},{6,5},{7,6},{8,7},{9,8},{10,9},{11,1... | collective-permute-start | bytes 1179656 | tf_op jit(solution)/shard_map/ppermute | solution.py:482

commit v5 on v4

--- a/solution.py
+++ b/solution.py
@@ -322,39 +322,74 @@
             out_ref[pl.ds(2 * pair + i, ensemble, stride=per), :] = mixed[:, i * LANES : (i + 1) * LANES]
 
 
-def advance_kernel(main_ref, low_ref, high_ref, out_ref, buf_ref, *, members, per):
+def each_member(one, members):
+    def some(i, _):
+        for r in range(UNROLL):
+            one(i * UNROLL + r, r)
+        return 0
+
+    lax.fori_loop(0, members // UNROLL, some, 0)
+
+
+def clear(buf_ref):
+    @pl.when(pl.program_id(0) == 0)
+    def _():
+        buf_ref[...] = jnp.zeros(buf_ref.shape, jnp.float32)
+
+
+def with_flux(parts, blocks):
+    return parts + [(1.0 + parts[cb]) * parts[2 * blocks + cb] for cb in range(blocks)]
+
+
+def loader(buf_ref, slot, blocks):
+    def load(f, shift):
+        return jnp.concatenate(
+            [buf_ref[slot, f * blocks + cb, 8 + shift : 16 + shift, :] for cb in range(blocks)], axis=1
+        )
+
+    return load
+
+
+def advance_kernel(main_ref, out_ref, buf_ref, *, members, per):
+    blocks = per // 3
+    stride = main_ref.shape[0] // 8
+    first = pl.program_id(0) * members
+    clear(buf_ref)
+
+    def one(i, slot):
+        parts = [main_ref[pl.ds((first + i) * per + j, 8, stride=stride), :] for j in range(per)]
+        for j, part in enumerate(with_flux(parts, blocks)):
+            buf_ref[slot, j, 8:16, :] = part
+        load = loader(buf_ref, slot, blocks)
+        slopes = tendency(load)
+        for f in range(3):
+            out_ref[i, f] = load(f, 0) + TIME_STEP * slopes[f]
+
+    each_member(one, members)
+
+
+def border_kernel(main_ref, low_ref, high_ref, part_ref, out_ref, buf_ref, *, members, per):
     blocks = per // 3
     here = main_ref.reshape(8 * members * per, LANES)
     stride = low_ref.shape[0] // 2
     first = pl.program_id(0) * members
+    clear(buf_ref)
 
     def one(i, slot):
-        m = first + i
-        for at, ref, count, row, apart in (
-            (6, low_ref, 2, m * per, stride),
-            (8, here, 8, i * per, members * per),
-            (16, high_ref, 2, m * per, stride),
-        ):
-            parts = [ref[pl.ds(row + j, count, stride=apart), :] for j in range(per)]
-            parts += [(1.0 + parts[cb]) * parts[2 * blocks + cb] for cb in range(blocks)]
-            for j, part in enumerate(parts):
-                buf_ref[slot, j, at : at + count, :] = part
-
-        def load(f, shift):
-            return jnp.concatenate(
-                [buf_ref[slot, f * blocks + cb, 8 + shift : 16 + shift, :] for cb in range(blocks)], axis=1
-            )
-
-        slopes = tendency(load)
+        at = (first + i) * per
+        for row, ref in ((6, low_ref), (16, high_ref)):
+            parts = [ref[pl.ds(at + j, 2, stride=stride), :] for j in range(per)]
+            for j, part in enumerate(with_flux(parts, blocks)):
+                buf_ref[slot, j, row : row + 2, :] = part
+        v = jnp.concatenate(
+            [here[pl.ds(i * per + 2 * blocks + cb, 8, stride=members * per), :] for cb in range(blocks)], axis=1
+        )
+        load = loader(buf_ref, slot, blocks)
+        rates = along_y(load, 3), v * along_y(load, 1), v * along_y(load, 2) + along_y(load, 0)
         for f in range(3):
-            out_ref[i, f] = load(f, 0) + TIME_STEP * slopes[f]
-
-    def some(i, _):
-        for r in range(UNROLL):
-            one(i * UNROLL + r, r)
-        return 0
-
-    lax.fori_loop(0, members // UNROLL, some, 0)
+            out_ref[i, f] = part_ref[i, f] - (TIME_STEP * SLOPE) * rates[f]
+
+    each_member(one, members)
 
 
 VMEM = pl.BlockSpec(memory_space=pltpu.VMEM)
@@ -440,17 +475,33 @@
     )(in_vmem(pieces), dev, in_vmem(mean))
 
 
-def advance(main, low, high, members, per):
+def advance(main, members, per):
     step = 8
     return pl.pallas_call(
         functools.partial(advance_kernel, members=step, per=per),
         grid=(members // step,),
-        in_specs=[pl.BlockSpec((8, step * per, LANES), lambda i: (0, i, 0)), VMEM, VMEM],
+        in_specs=[VMEM],
         out_specs=pl.BlockSpec((step, 3, 8, per // 3 * LANES), lambda i: (i, 0, 0, 0)),
         out_shape=f32(members, 3, 8, per // 3 * LANES),
         scratch_shapes=[pltpu.VMEM((UNROLL, per // 3 * 4, 24, LANES), jnp.float32)],
+        cost_estimate=pl.CostEstimate(flops=1 << 28, transcendentals=0, bytes_accessed=1 << 22),
         name="advance",
-    )(main.reshape(8, members * per, LANES), in_vmem(low), in_vmem(high))
+    )(in_vmem(main))
+
+
+def add_border(main, low, high, partial, members, per):
+    step = 8
+    block = pl.BlockSpec((step, 3, 8, per // 3 * LANES), lambda i: (i, 0, 0, 0))
+    return pl.pallas_call(
+        functools.partial(border_kernel, members=step, per=per),
+        grid=(members // step,),
+        in_specs=[pl.BlockSpec((8, step * per, LANES), lambda i: (0, i, 0)), VMEM, VMEM, block],
+        out_specs=block,
+        out_shape=f32(members, 3, 8, per // 3 * LANES),
+        scratch_shapes=[pltpu.VMEM((UNROLL, per // 3 * 4, 24, LANES), jnp.float32)],
+        input_output_aliases={3: 0},
+        name="border",
+    )(main.reshape(8, members * per, LANES), in_vmem(low), in_vmem(high), partial)
 
 
 def exchange(rows, axes, count):
@@ -480,7 +531,8 @@
     backward = [(target, source) for source, target in forward]
     low = lax.ppermute(analysed[-edge:], "tile", forward)
     high = lax.ppermute(analysed[:edge], "tile", backward)
-    return advance(analysed, low, high, members_dev, per)
+    partial = advance(analysed, members_dev, per)
+    return add_border(analysed, low, high, partial, members_dev, per)
 
 
 def solution(mesh):

time: 165 us -> 165 us (level)
  waiting for transfers between devices: 8.47 us -> 4.67 us
  Pallas kernels: 36.8 us -> 39.9 us
    pallas_call x0 -> x1, Pallas kernels: none -> 4.56 us  [add_border(): pl.pallas_call(functools.partial(border_kernel, members=step, per=per), g...]
    ppermute x1, waiting for transfers between devices: 8.46 us -> 4.67 us  [per_device(): low = lax.ppermute(analysed[-edge:], 'tile', forward)]
  transfers between devices with their start and end apart: 2 -> 2, of which waited for: 1 -> 1; matrix products, arithmetic and copies ran while one was open for 0% -> 0% of each run, Pallas kernels for 0% -> 2%
where the time goes in v5:
time: 165 us; the launch traced here: 164 us
  blocking collectives  114 us (69%)
  Pallas kernels  39.9 us (24%)
  starting transfers between devices  5.41 us (3%)
  waiting for transfers between devices  4.67 us (3%)
    all_to_all x5, blocking collectives, exchange(): moved = lax.all_to_all(rows.reshape(count, -1), axes, 0, 0, tiled=True)  114 us
    pallas_call x1, Pallas kernels, analyse(): pl.pallas_call(functools.partial(root_kernel, ensemble=ensemble, per=per)...  14.4 us
    pallas_call x1, Pallas kernels, runge_kutta(): pl.pallas_call(functools.partial(runge_kutta_kernel, tiles=tiles, members...  11.5 us
    ppermute x1, starting transfers between devices, per_device(): high = lax.ppermute(analysed[:edge], 'tile', backward)  4.76 us
    ppermute x1, waiting for transfers between devices, per_device(): low = lax.ppermute(analysed[-edge:], 'tile', forward)  4.67 us
    pallas_call x1, Pallas kernels, add_border(): pl.pallas_call(functools.partial(border_kernel, members=step, per=per), g...  4.56 us
    pallas_call x1, Pallas kernels, gram_pieces(): pl.pallas_call(functools.partial(gram_kernel, ensemble=ensemble, per=per)...  4.19 us
    pallas_call x1, Pallas kernels, advance(): pl.pallas_call(functools.partial(advance_kernel, members=step, per=per),...  3.79 us
  transfers between devices with their start and end apart: 2, of which 1 were waited for; matrix products, arithmetic and copies ran while one was open for 0% of the time, Pallas kernels for 2%

profile of v5, /device:TPU:0, one launch (start us, length us, event | category | flops | bytes accessed | tf_op | source)
XLA Modules:
  0.0 164.3 jit_solution(4577809582829935189)
XLA Ops:
  0.0 1.5 start.1
  1.5 29.7 %all_to_all.45 = f32[16,1,24576]{2,1,0:T(1,128)S(1)} all-to-all(f32[16,1,24576]{2,1,0:T(1,128)S(1)} %bitcast.22), channel_id=1, replica_groups=mesh['runner'=8,'tile'=16] {'tile'}, dimensions={0} | all-to-all | bytes 3145728 | tf_op jit(solution)/shard_map/all_to_all | solution.py:508
  31.2 11.5 %runge_kutta.1 = f32[3072,128]{1,0:T(8,128)S(1)} custom-call(f32[3072,128]{1,0:T(8,128)S(1)} %bitcast.20), custom_call_target="tpu_custom_call" | custom-call | tf_op jit(solution)/shard_map/runge_kutta/pallas_call | solution.py:429
  42.7 31.4 %all_to_all.46 = f32[128,1,3072]{2,1,0:T(1,128)S(1)} all-to-all(f32[128,1,3072]{2,1,0:T(1,128)S(1)} %bitcast.21), channel_id=1, replica_groups=mesh['runner'=8,'tile'=16] {'runner','tile'}, dimensions={0} | all-to-all | bytes 3145728 | tf_op jit(solution)/shard_map/all_to_all | solution.py:508
  74.1 4.2 %gram.1 = (f32[384,128]{1,0:T(8,128)S(1)}, f32[256,1536]{1,0:T(8,128)}, f32[8,1536]{1,0:T(8,128)S(1)}) custom-call(f32[3072,128]{1,0:T(8,128)S(1)} %bitcast.18, s32[1,256]{1,0:T(1,128)} %bitcast.29, f32[1,256]{1,0:T(1,128)} %bitcast.30, f32[1,256]{1,0:T(1,128)} %bitcast.31), custom_call_target="tpu_custom_call" | custom-call | tf_op jit(solution)/shard_map/gram/pallas_call | solution.py:444
  78.3 14.4 %all_to_all.47 = f32[128,1,384]{2,1,0:T(1,128)S(1)} all-to-all(f32[128,1,384]{2,1,0:T(1,128)S(1)} %bitcast.26), channel_id=1, replica_groups=mesh['runner'=8,'tile'=16] {'runner','tile'}, dimensions={0} | all-to-all | bytes 393216 | tf_op jit(solution)/shard_map/all_to_all | solution.py:508
  92.8 14.6 %all_to_all.48 = f32[128,1,384]{2,1,0:T(1,128)S(1)} all-to-all(f32[128,1,384]{2,1,0:T(1,128)S(1)} %bitcast.25), channel_id=1, replica_groups=mesh['runner'=8,'tile'=16] {'runner','tile'}, dimensions={0} | all-to-all | bytes 393216 | tf_op jit(solution)/shard_map/all_to_all | solution.py:508
  107.4 14.4 %analyse.1 = f32[3072,128]{1,0:T(8,128)S(1)} custom-call(f32[384,128]{1,0:T(8,128)S(1)} %bitcast.23, f32[256,1536]{1,0:T(8,128)} %get-tuple-element.9.dev_ref, f32[8,1536]{1,0:T(8,128)S(1)} %get-tuple-element.10.mean_ref), custom_call_target="tpu_custom_call" | custom-call | tf_op jit(solution)/shard_map/analyse/pallas_call | solution.py:464
  121.8 24.0 %all_to_all.49 = f32[8,1,49152]{2,1,0:T(1,128)S(1)} all-to-all(f32[8,1,49152]{2,1,0:T(1,128)S(1)} %bitcast.19), channel_id=1, replica_groups=mesh['runner'=8,'tile'=16] {'runner'}, dimensions={0} | all-to-all | bytes 3145728 | tf_op jit(solution)/shard_map/all_to_all | solution.py:508
  145.8 0.0 copy-start
  145.8 0.1 fusion
  145.8 0.7 collective-permute-start
  146.5 4.8 %collective-permute-start.1 = (f32[768,128]{1,0:T(8,128)S(1)}, f32[768,128]{1,0:T(8,128)S(1)}, u32[]{:S(2)}, u32[]{:S(2)}) collective-permute-start(f32[768,128]{1,0:T(8,128)S(1)} %bitcast.27), channel_id=1, source_target_pairs={{1,0},{2,1},{3,2},{4,3},{5,4},{6,5},{7,6},{8,7},{9,8},{10,9},{11,1... | collective-permute-start | bytes 1179656 | tf_op jit(solution)/shard_map/ppermute | solution.py:533
  151.3 3.8 %advance.1.part_ref = f32[32,3,8,512]{3,2,1,0:T(8,128)} custom-call(f32[3072,128]{1,0:T(8,128)S(1)} %bitcast.16), custom_call_target="tpu_custom_call" | custom-call | flops 268435456 | bytes 4194304 | tf_op jit(solution)/shard_map/advance/pallas_call | solution.py:480
  155.1 0.0 copy-done
  155.1 4.7 %collective-permute-done.low_ref = f32[768,128]{1,0:T(8,128)S(1)} collective-permute-done((f32[768,128]{1,0:T(8,128)S(1)}, f32[768,128]{1,0:T(8,128)S(1)}, u32[]{:S(2)}, u32[]{:S(2)}) %collective-permute-start) | collective-permute-done | bytes 393248 | tf_op jit(solution)/shard_map/ppermute | solution.py:532
  159.7 0.0 collective-permute-done.1.high_ref
  159.7 4.6 %border.1 = f32[32,3,8,512]{3,2,1,0:T(8,128)} custom-call(f32[8,384,128]{2,1,0:T(8,128)} %bitcast.17, f32[768,128]{1,0:T(8,128)S(1)} %collective-permute-done.low_ref, f32[768,128]{1,0:T(8,128)S(1)} %collective-permute-done.1.high_ref, f32[32,3,8,512]{3,2,1,0:T(8,128)} %advance.1.part_ref), custom_call_target="tpu_custom_call", output_to_operand_aliasing={{}: (3, {})} | custom-call | tf_op jit(solution)/shard_map/border/pallas_call | solution.py:495
  (1 shorter events, 0.0 us)
Async XLA Ops:
  145.8 9.3 %copy-start = (f32[8,1,49152]{2,1,0:T(1,128)}, f32[8,1,49152]{2,1,0:T(1,128)S(1)}, u32[]{:S(2)}) copy-start(f32[8,1,49152]{2,1,0:T(1,128)S(1)} %all_to_all.49) | copy-start | bytes 4718596
  145.8 13.9 %collective-permute-start = (f32[768,128]{1,0:T(8,128)S(1)}, f32[768,128]{1,0:T(8,128)S(1)}, u32[]{:S(2)}, u32[]{:S(2)}) collective-permute-start(f32[768,128]{1,0:T(8,128)S(1)} %bitcast.28), channel_id=1, source_target_pairs={{0,1},{1,2},{2,3},{3,4},{4,5},{5,6},{6,7},{7,8},{8,9},{9,10},{10,1... | collective-permute-start | bytes 1179656 | tf_op jit(solution)/shard_map/ppermute | solution.py:532
  146.5 13.2 %collective-permute-start.1 = (f32[768,128]{1,0:T(8,128)S(1)}, f32[768,128]{1,0:T(8,128)S(1)}, u32[]{:S(2)}, u32[]{:S(2)}) collective-permute-start(f32[768,128]{1,0:T(8,128)S(1)} %bitcast.27), channel_id=1, source_target_pairs={{1,0},{2,1},{3,2},{4,3},{5,4},{6,5},{7,6},{8,7},{9,8},{10,9},{11,1... | collective-permute-start | bytes 1179656 | tf_op jit(solution)/shard_map/ppermute | solution.py:533

commit v6 on v5

--- a/solution.py
+++ b/solution.py
@@ -61,6 +61,7 @@
 
 
 UNROLL = 4
+RK_UNROLL = 16
 
 
 def runge_kutta_kernel(in_ref, out_ref, even_ref, odd_ref, acc_ref, *, tiles, members, blocks):
@@ -73,11 +74,11 @@
 
     def every_tile(step):
         def some(i, _):
-            for r in range(UNROLL):
-                step(i * UNROLL + r)
+            for r in range(RK_UNROLL):
+                step(i * RK_UNROLL + r)
             return 0
 
-        lax.fori_loop(0, tiles // UNROLL, some, 0)
+        lax.fori_loop(0, tiles // RK_UNROLL, some, 0)
 
     def member_step(m, _):
         def start_of(t, f):
@@ -167,11 +168,12 @@
         lanes = slice(pair * 2 * LANES, (pair + 1) * 2 * LANES)
         copies.append(pltpu.make_async_copy(buf_ref.at[:, lanes], dev_ref.at[:, lanes], sem_ref.at[pair]))
         copies[-1].start()
+        x1, x2, x3 = split3(jnp.concatenate(lefts, axis=1))
+        y1, y2, y3 = split3(jnp.concatenate(devs, axis=1))
         total = total + lax.dot_general(
-            jnp.concatenate(lefts, axis=1),
-            jnp.concatenate(devs, axis=1),
+            jnp.concatenate([x1, x1, x2, x2, x1, x3], axis=1),
+            jnp.concatenate([y1, y2, y1, y2, y3, y1], axis=1),
             (((1,), (1,)), ((), ())),
-            precision=lax.Precision.HIGHEST,
             preferred_element_type=jnp.float32,
         )
     half = ensemble // 2
@@ -284,40 +286,47 @@
         own = (lane_wide >= k * BLOCK) & (lane_wide < (k + 1) * BLOCK)
         minus_eye = jnp.where(lane_wide == row_wide + k * BLOCK, -1.0, 0.0)
         bars = [jnp.where(own, minus_eye, r) for r in rows]
+        l1, l2, l3 = split3(left)
+        b1, b2, b3 = split3(jnp.concatenate(bars, axis=0))
         swept = jnp.dot(
-            left,
-            jnp.concatenate(bars, axis=0),
-            precision=lax.Precision.HIGHEST,
+            jnp.concatenate([l1, l1, l2, l2, l1, l3], axis=1),
+            jnp.concatenate([b1, b2, b1, b2, b3, b1], axis=0),
             preferred_element_type=jnp.float32,
         )
+        own_all = (lane_id >= k * BLOCK) & (lane_id < (k + 1) * BLOCK)
+        stacked = []
         for s in range(shifts):
             z = swept[s * BLOCK : (s + 1) * BLOCK, :]
             y1, y2, y3 = split3(jnp.where(own, 0.0, z))
-            r1, r2, r3 = split3(bars[s])
-            update = lax.dot_general(
-                jnp.concatenate([y1, y1, y2, y2, y1, y3], axis=0),
-                jnp.concatenate([r1, r2, r1, r2, r3, r1], axis=0),
-                (((0,), (0,)), ((), ())),
-                preferred_element_type=jnp.float32,
+            r1, r2, r3 = (b[s * BLOCK : (s + 1) * BLOCK, :] for b in (b1, b2, b3))
+            stacked.append(
+                (jnp.concatenate([y1, y1, y2, y2, y1, y3], axis=0), jnp.concatenate([r1, r2, r1, r2, r3, r1], axis=0))
             )
-            own_all = (lane_id >= k * BLOCK) & (lane_id < (k + 1) * BLOCK)
-            work_ref[s] = jnp.where(own_all, 0.0, work_ref[s]) - update
-            work_ref[s, k * BLOCK : (k + 1) * BLOCK, :] = z
+        ahead = (k + 1) * BLOCK // half % 2
+        for side in (ahead, 1 - ahead):
+            here = slice(side * half, (side + 1) * half)
+            for s, (y, r) in enumerate(stacked):
+                update = lax.dot_general(
+                    y[:, here], r, (((0,), (0,)), ((), ())), preferred_element_type=jnp.float32
+                )
+                work_ref[s, here, :] = jnp.where(own_all[here], 0.0, work_ref[s, here, :]) - update
+        for s in range(shifts):
+            work_ref[s, k * BLOCK : (k + 1) * BLOCK, :] = swept[s * BLOCK : (s + 1) * BLOCK, :]
     root = jnp.where(diag, ROOT_CONST, 0.0)
     for s in range(shifts):
         root = root - ROOT_COEF[s] * work_ref[s]
     inner = jnp.sum(root * innovation, axis=1, keepdims=True)
     weights = jnp.sum(root * inner, axis=0, keepdims=True) * (1.0 / (ensemble - 1.0))
     mixing = root + weights
+    m1, m2, m3 = split3(mixing)
+    mixing6 = jnp.concatenate([m1, m1, m2, m2, m1, m3], axis=1)
     fetch.wait()
     for pair in range(per // 2):
         lanes = slice(pair * 2 * LANES, (pair + 1) * 2 * LANES)
-        mixed = jnp.dot(
-            mixing,
-            buf_ref[:, lanes],
-            precision=lax.Precision.HIGHEST,
-            preferred_element_type=jnp.float32,
-        ) + mean_ref[0:1, lanes]
+        d1, d2, d3 = split3(buf_ref[:, lanes])
+        mixed = mean_ref[0:1, lanes] + jnp.dot(
+            mixing6, jnp.concatenate([d1, d2, d1, d2, d3, d1], axis=0), preferred_element_type=jnp.float32
+        )
         for i in range(2):
             out_ref[pl.ds(2 * pair + i, ensemble, stride=per), :] = mixed[:, i * LANES : (i + 1) * LANES]
 
@@ -350,7 +359,7 @@
     return load
 
 
-def advance_kernel(main_ref, out_ref, buf_ref, *, members, per):
+def advance_kernel(main_ref, out_ref, north_ref, buf_ref, *, members, per):
     blocks = per // 3
     stride = main_ref.shape[0] // 8
     first = pl.program_id(0) * members
@@ -360,6 +369,8 @@
         parts = [main_ref[pl.ds((first + i) * per + j, 8, stride=stride), :] for j in range(per)]
         for j, part in enumerate(with_flux(parts, blocks)):
             buf_ref[slot, j, 8:16, :] = part
+        for cb in range(blocks):
+            north_ref[i, cb] = parts[2 * blocks + cb]
         load = loader(buf_ref, slot, blocks)
         slopes = tendency(load)
         for f in range(3):
@@ -368,9 +379,8 @@
     each_member(one, members)
 
 
-def border_kernel(main_ref, low_ref, high_ref, part_ref, out_ref, buf_ref, *, members, per):
+def border_kernel(north_ref, low_ref, high_ref, part_ref, out_ref, buf_ref, *, members, per):
     blocks = per // 3
-    here = main_ref.reshape(8 * members * per, LANES)
     stride = low_ref.shape[0] // 2
     first = pl.program_id(0) * members
     clear(buf_ref)
@@ -381,9 +391,7 @@
             parts = [ref[pl.ds(at + j, 2, stride=stride), :] for j in range(per)]
             for j, part in enumerate(with_flux(parts, blocks)):
                 buf_ref[slot, j, row : row + 2, :] = part
-        v = jnp.concatenate(
-            [here[pl.ds(i * per + 2 * blocks + cb, 8, stride=members * per), :] for cb in range(blocks)], axis=1
-        )
+        v = jnp.concatenate([north_ref[i, cb] for cb in range(blocks)], axis=1)
         load = loader(buf_ref, slot, blocks)
         rates = along_y(load, 3), v * along_y(load, 1), v * along_y(load, 2) + along_y(load, 0)
         for f in range(3):
@@ -481,27 +489,30 @@
         functools.partial(advance_kernel, members=step, per=per),
         grid=(members // step,),
         in_specs=[VMEM],
-        out_specs=pl.BlockSpec((step, 3, 8, per // 3 * LANES), lambda i: (i, 0, 0, 0)),
-        out_shape=f32(members, 3, 8, per // 3 * LANES),
+        out_specs=[
+            pl.BlockSpec((step, 3, 8, per // 3 * LANES), lambda i: (i, 0, 0, 0)),
+            pl.BlockSpec((step, per // 3, 8, LANES), lambda i: (i, 0, 0, 0)),
+        ],
+        out_shape=[f32(members, 3, 8, per // 3 * LANES), f32(members, per // 3, 8, LANES)],
         scratch_shapes=[pltpu.VMEM((UNROLL, per // 3 * 4, 24, LANES), jnp.float32)],
         cost_estimate=pl.CostEstimate(flops=1 << 28, transcendentals=0, bytes_accessed=1 << 22),
         name="advance",
     )(in_vmem(main))
 
 
-def add_border(main, low, high, partial, members, per):
-    step = 8
+def add_border(north, low, high, partial, members, per):
+    step = 16
     block = pl.BlockSpec((step, 3, 8, per // 3 * LANES), lambda i: (i, 0, 0, 0))
     return pl.pallas_call(
         functools.partial(border_kernel, members=step, per=per),
         grid=(members // step,),
-        in_specs=[pl.BlockSpec((8, step * per, LANES), lambda i: (0, i, 0)), VMEM, VMEM, block],
+        in_specs=[pl.BlockSpec((step, per // 3, 8, LANES), lambda i: (i, 0, 0, 0)), VMEM, VMEM, block],
         out_specs=block,
         out_shape=f32(members, 3, 8, per // 3 * LANES),
         scratch_shapes=[pltpu.VMEM((UNROLL, per // 3 * 4, 24, LANES), jnp.float32)],
         input_output_aliases={3: 0},
         name="border",
-    )(main.reshape(8, members * per, LANES), in_vmem(low), in_vmem(high), partial)
+    )(north, in_vmem(low), in_vmem(high), partial)
 
 
 def exchange(rows, axes, count):
@@ -531,8 +542,8 @@
     backward = [(target, source) for source, target in forward]
     low = lax.ppermute(analysed[-edge:], "tile", forward)
     high = lax.ppermute(analysed[:edge], "tile", backward)
-    partial = advance(analysed, members_dev, per)
-    return add_border(analysed, low, high, partial, members_dev, per)
+    partial, north = advance(analysed, members_dev, per)
+    return add_border(north, low, high, partial, members_dev, per)
 
 
 def solution(mesh):

time: 165 us -> 160 us (0.970)
  Pallas kernels: 39.9 us -> 35.2 us
    pallas_call x1, Pallas kernels: 11.5 us -> 9.07 us  [runge_kutta(): pl.pallas_call(functools.partial(runge_kutta_kernel, tiles=tiles, members...]
where the time goes in v6:
time: 160 us; the launch traced here: 159 us
  blocking collectives  114 us (71%)
  Pallas kernels  35.2 us (22%)
  starting transfers between devices  5.41 us (3%)
  waiting for transfers between devices  4.61 us (3%)
    all_to_all x5, blocking collectives, exchange(): moved = lax.all_to_all(rows.reshape(count, -1), axes, 0, 0, tiled=True)  114 us
    pallas_call x1, Pallas kernels, analyse(): pl.pallas_call(functools.partial(root_kernel, ensemble=ensemble, per=per)...  13.2 us
    pallas_call x1, Pallas kernels, runge_kutta(): pl.pallas_call(functools.partial(runge_kutta_kernel, tiles=tiles, members...  9.07 us
    ppermute x1, starting transfers between devices, per_device(): high = lax.ppermute(analysed[:edge], 'tile', backward)  4.74 us
    ppermute x1, waiting for transfers between devices, per_device(): low = lax.ppermute(analysed[-edge:], 'tile', forward)  4.61 us
    pallas_call x1, Pallas kernels, gram_pieces(): pl.pallas_call(functools.partial(gram_kernel, ensemble=ensemble, per=per)...  4.01 us
    pallas_call x1, Pallas kernels, advance(): pl.pallas_call(functools.partial(advance_kernel, members=step, per=per),...  3.85 us
    pallas_call x1, Pallas kernels, add_border(): pl.pallas_call(functools.partial(border_kernel, members=step, per=per), g...  3.53 us
  transfers between devices with their start and end apart: 2, of which 1 were waited for; matrix products, arithmetic and copies ran while one was open for 0% of the time, Pallas kernels for 2%

profile of v6, /device:TPU:0, one launch (start us, length us, event | category | flops | bytes accessed | tf_op | source)
XLA Modules:
  0.0 159.5 jit_solution(18402542308765228558)
XLA Ops:
  0.0 1.5 start.1
  1.5 29.7 %all_to_all.45 = f32[16,1,24576]{2,1,0:T(1,128)S(1)} all-to-all(f32[16,1,24576]{2,1,0:T(1,128)S(1)} %bitcast.20), channel_id=1, replica_groups=mesh['runner'=8,'tile'=16] {'tile'}, dimensions={0} | all-to-all | bytes 3145728 | tf_op jit(solution)/shard_map/all_to_all | solution.py:519
  31.2 9.1 %runge_kutta.1 = f32[3072,128]{1,0:T(8,128)S(1)} custom-call(f32[3072,128]{1,0:T(8,128)S(1)} %bitcast.18), custom_call_target="tpu_custom_call" | custom-call | tf_op jit(solution)/shard_map/runge_kutta/pallas_call | solution.py:437
  40.3 31.4 %all_to_all.46 = f32[128,1,3072]{2,1,0:T(1,128)S(1)} all-to-all(f32[128,1,3072]{2,1,0:T(1,128)S(1)} %bitcast.19), channel_id=1, replica_groups=mesh['runner'=8,'tile'=16] {'runner','tile'}, dimensions={0} | all-to-all | bytes 3145728 | tf_op jit(solution)/shard_map/all_to_all | solution.py:519
  71.7 4.0 %gram.1 = (f32[384,128]{1,0:T(8,128)S(1)}, f32[256,1536]{1,0:T(8,128)}, f32[8,1536]{1,0:T(8,128)S(1)}) custom-call(f32[3072,128]{1,0:T(8,128)S(1)} %bitcast.16, s32[1,256]{1,0:T(1,128)} %bitcast.27, f32[1,256]{1,0:T(1,128)} %bitcast.28, f32[1,256]{1,0:T(1,128)} %bitcast.29), custom_call_target="tpu_custom_call" | custom-call | tf_op jit(solution)/shard_map/gram/pallas_call | solution.py:452
  75.7 14.4 %all_to_all.47 = f32[128,1,384]{2,1,0:T(1,128)S(1)} all-to-all(f32[128,1,384]{2,1,0:T(1,128)S(1)} %bitcast.24), channel_id=1, replica_groups=mesh['runner'=8,'tile'=16] {'runner','tile'}, dimensions={0} | all-to-all | bytes 393216 | tf_op jit(solution)/shard_map/all_to_all | solution.py:519
  90.1 14.6 %all_to_all.48 = f32[128,1,384]{2,1,0:T(1,128)S(1)} all-to-all(f32[128,1,384]{2,1,0:T(1,128)S(1)} %bitcast.23), channel_id=1, replica_groups=mesh['runner'=8,'tile'=16] {'runner','tile'}, dimensions={0} | all-to-all | bytes 393216 | tf_op jit(solution)/shard_map/all_to_all | solution.py:519
  104.7 13.2 %analyse.1 = f32[3072,128]{1,0:T(8,128)S(1)} custom-call(f32[384,128]{1,0:T(8,128)S(1)} %bitcast.21, f32[256,1536]{1,0:T(8,128)} %get-tuple-element.11.dev_ref, f32[8,1536]{1,0:T(8,128)S(1)} %get-tuple-element.12.mean_ref), custom_call_target="tpu_custom_call" | custom-call | tf_op jit(solution)/shard_map/analyse/pallas_call | solution.py:472
  118.0 24.0 %all_to_all.49 = f32[8,1,49152]{2,1,0:T(1,128)S(1)} all-to-all(f32[8,1,49152]{2,1,0:T(1,128)S(1)} %bitcast.17), channel_id=1, replica_groups=mesh['runner'=8,'tile'=16] {'runner'}, dimensions={0} | all-to-all | bytes 3145728 | tf_op jit(solution)/shard_map/all_to_all | solution.py:519
  142.0 0.1 fusion
  142.1 0.7 collective-permute-start
  142.7 4.7 %collective-permute-start.1 = (f32[768,128]{1,0:T(8,128)S(1)}, f32[768,128]{1,0:T(8,128)S(1)}, u32[]{:S(2)}, u32[]{:S(2)}) collective-permute-start(f32[768,128]{1,0:T(8,128)S(1)} %bitcast.25), channel_id=1, source_target_pairs={{1,0},{2,1},{3,2},{4,3},{5,4},{6,5},{7,6},{8,7},{9,8},{10,9},{11,1... | collective-permute-start | bytes 1179656 | tf_op jit(solution)/shard_map/ppermute | solution.py:544
  147.5 3.9 %advance.1 = (f32[32,3,8,512]{3,2,1,0:T(8,128)}, f32[32,4,8,128]{3,2,1,0:T(8,128)}) custom-call(f32[3072,128]{1,0:T(8,128)S(1)} %bitcast.15), custom_call_target="tpu_custom_call" | custom-call | flops 268435456 | bytes 4194304 | tf_op jit(solution)/shard_map/advance/pallas_call | solution.py:488
  151.3 4.6 %collective-permute-done.low_ref = f32[768,128]{1,0:T(8,128)S(1)} collective-permute-done((f32[768,128]{1,0:T(8,128)S(1)}, f32[768,128]{1,0:T(8,128)S(1)}, u32[]{:S(2)}, u32[]{:S(2)}) %collective-permute-start) | collective-permute-done | bytes 393248 | tf_op jit(solution)/shard_map/ppermute | solution.py:543
  155.9 0.0 collective-permute-done.1.high_ref
  155.9 3.5 %border.1 = f32[32,3,8,512]{3,2,1,0:T(8,128)} custom-call(f32[32,4,8,128]{3,2,1,0:T(8,128)} %get-tuple-element.13.north_ref, f32[768,128]{1,0:T(8,128)S(1)} %collective-permute-done.low_ref, f32[768,128]{1,0:T(8,128)S(1)} %collective-permute-done.1.high_ref, f32[32,3,8,512]{3,2,1,0:T(8,128)} %get-tuple-element.14.part_ref), custom_call_target="tpu_custom_call", output_to_operand_aliasing={{}: (3, {})} | custom-call | tf_op jit(solution)/shard_map/border/pallas_call | solution.py:506
  (1 shorter events, 0.0 us)
Async XLA Ops:
  142.1 13.9 %collective-permute-start = (f32[768,128]{1,0:T(8,128)S(1)}, f32[768,128]{1,0:T(8,128)S(1)}, u32[]{:S(2)}, u32[]{:S(2)}) collective-permute-start(f32[768,128]{1,0:T(8,128)S(1)} %bitcast.26), channel_id=1, source_target_pairs={{0,1},{1,2},{2,3},{3,4},{4,5},{5,6},{6,7},{7,8},{8,9},{9,10},{10,1... | collective-permute-start | bytes 1179656 | tf_op jit(solution)/shard_map/ppermute | solution.py:543
  142.7 13.2 %collective-permute-start.1 = (f32[768,128]{1,0:T(8,128)S(1)}, f32[768,128]{1,0:T(8,128)S(1)}, u32[]{:S(2)}, u32[]{:S(2)}) collective-permute-start(f32[768,128]{1,0:T(8,128)S(1)} %bitcast.25), channel_id=1, source_target_pairs={{1,0},{2,1},{3,2},{4,3},{5,4},{6,5},{7,6},{8,7},{9,8},{10,9},{11,1... | collective-permute-start | bytes 1179656 | tf_op jit(solution)/shard_map/ppermute | solution.py:544
